TPU v7x, 128 devices: a whole 4x4x4 slice. The times are simulated.
128 devices in a mesh: gz: 2 (over x_lo), gx: 2 (over core), gy: 32 (over z, y, x_hi).
Axes of the slice: x: 4 (x_hi: 2, x_lo: 2; x = x_hi * 2 + x_lo), y: 4, z: 4, core: 2. Of those that a mesh axis runs over, the one named last changes fastest.
Arguments:
- initial_field: float32 [128, 16, 4096], P('gz', 'gx', 'gy'), may hold values from -36 to 36
- plane_coupling: float32 [128, 16, 4096], P('gz', 'gx', 'gy'), may hold values from 0.06 to 0.24
- line_coupling: float32 [128, 16, 4096], P('gz', 'gx', 'gy'), may hold values from 1000 to 8000
- source: float32 [128, 16, 4096], P('gz', 'gx', 'gy'), may hold values from -4 to 4, as said below
- shift_table: float32 [8], replicated, may hold values from 0.5 to 1
- shift_index: int32 [4], replicated, may hold values from 0 to 7
Outputs:
- heated: float32 [128, 16, 4096], P('gz', 'gx', 'gy')
Inputs may be any that keep to these rules, and one draw needn't show every extreme that they name: `shift_index`: one table row for each half-step. A heat source.
All inputs are finite; a program needn't handle non-finite values.
Results may differ from a plain program's by a relative error of at most 0.0003.
Values sent between devices are 32-bit elements; how exact they have to be, the bound alone decides.
A program may use at most 64 MiB of HBM per device.

v0:
```python
import jax
import jax.numpy as jnp
from jax import lax
from jax.sharding import PartitionSpec as P

HALF = 4


def joined_along(parts, dim):
    shape = list(parts.shape[1:])
    shape[dim] *= parts.shape[0]
    return jnp.moveaxis(parts, 0, dim).reshape(shape)


def copy_for_each(x, axis):
    copies = jnp.broadcast_to(x, (lax.axis_size(axis), *x.shape))
    return lax.all_to_all(copies, axis, split_axis=0, concat_axis=0, tiled=True)


def gathered_copies(x, axis, dim):
    return joined_along(copy_for_each(x, axis), dim)


def side_by_side(arrays, axis, dim, along):
    ends, at = ([], 0)
    for a in arrays[:-1]:
        at += a.shape[along]
        ends.append(at)
    both = jnp.concatenate(arrays, axis=along)
    return tuple(jnp.split(gathered_copies(both, axis, dim), ends, axis=along))


def padded_2(x, sides, width):
    edges = {}
    for axis, dim in sides:
        size, length = (lax.axis_size(axis), x.shape[dim])
        up = [(i, (i + 1) % size) for i in range(size - 1)]
        last = lax.slice_in_dim(x, length - width, length, axis=dim)
        first = lax.slice_in_dim(x, 0, width, axis=dim)
        edges[dim] = (
            lax.ppermute(last, axis, up),
            lax.ppermute(first, axis, [(b, a) for a, b in up]),
        )
    done = []
    for _, dim in sides:
        low, high = edges[dim]
        around = [(width, width) if d in done else (0, 0) for d in range(x.ndim)]
        x = jnp.concatenate([jnp.pad(low, around), x, jnp.pad(high, around)], axis=dim)
        done.append(dim)
    return x


def lookup(shift_table, table_row):
    table_slots = jnp.arange(shift_table.shape[0], dtype=jnp.int32)
    return jnp.sum(jnp.where(table_slots == table_row, shift_table, jnp.zeros_like(shift_table)))


def from_below(values, stride, fill_value, which_axis):
    filler_shape = list(values.shape)
    filler_shape[which_axis] = stride
    filler = jnp.full(filler_shape, fill_value, values.dtype)
    retained = lax.slice_in_dim(values, 0, values.shape[which_axis] - stride, axis=which_axis)
    return jnp.concatenate([filler, retained], axis=which_axis)


def from_above(values, stride, fill_value, which_axis):
    filler_shape = list(values.shape)
    filler_shape[which_axis] = stride
    filler = jnp.full(filler_shape, fill_value, values.dtype)
    retained = lax.slice_in_dim(values, stride, values.shape[which_axis], axis=which_axis)
    return jnp.concatenate([retained, filler], axis=which_axis)


def local_solve(scaled, forcing):
    lower_band = -scaled
    upper_band = -scaled
    main_band = 1.0 + 2.0 * scaled
    layer_count = scaled.shape[0]
    stride = 1
    while stride < layer_count:
        lower_before = from_below(lower_band, stride, 0.0, 0)
        main_before = from_below(main_band, stride, 1.0, 0)
        upper_before = from_below(upper_band, stride, 0.0, 0)
        forcing_before = from_below(forcing, stride, 0.0, 1)
        lower_after = from_above(lower_band, stride, 0.0, 0)
        main_after = from_above(main_band, stride, 1.0, 0)
        upper_after = from_above(upper_band, stride, 0.0, 0)
        forcing_after = from_above(forcing, stride, 0.0, 1)
        left_factor = -lower_band / main_before
        right_factor = -upper_band / main_after
        main_band = main_band + left_factor * upper_before + right_factor * lower_after
        forcing = forcing + left_factor * forcing_before + right_factor * forcing_after
        lower_band = left_factor * lower_before
        upper_band = right_factor * upper_after
        stride = stride * 2
    return forcing / main_band


def reduced_gathered(first_y, last_y, first_f, last_f, first_g, last_g):
    gathered = side_by_side(
        (first_y[None], last_y[None], first_f[None], last_f[None], first_g[None], last_g[None]),
        "gz",
        0,
        1,
    )
    zero_plane = jnp.zeros_like(first_y)

    def forward(previous, entries):
        offset, slope_part = previous
        start_y, end_y, start_f, end_f, start_g, end_g = entries
        pivot_value = 1.0 - start_f * slope_part
        constant = (start_y + start_f * offset) / pivot_value
        factor = start_g / pivot_value
        next_offset = end_y + end_f * (offset + slope_part * start_y) / pivot_value
        next_slope = end_g + end_f * slope_part * start_g / pivot_value
        return ((next_offset, next_slope), (offset, slope_part, constant, factor))

    final_state, outcome = lax.scan(forward, (zero_plane, zero_plane), gathered)
    offsets, slopes, constants, factors = outcome

    def backward(later_value, entries):
        constant, factor = entries
        own_value = constant + factor * later_value
        return (own_value, (own_value, later_value))

    final_value, solved = lax.scan(backward, zero_plane, (constants, factors), reverse=True)
    own_values, next_values = solved
    device = lax.axis_index("gz")
    offset = lax.dynamic_index_in_dim(offsets, device, 0, keepdims=False)
    slope_part = lax.dynamic_index_in_dim(slopes, device, 0, keepdims=False)
    own_value = lax.dynamic_index_in_dim(own_values, device, 0, keepdims=False)
    next_value = lax.dynamic_index_in_dim(next_values, device, 0, keepdims=False)
    return (offset + slope_part * own_value, next_value)


def on_device(initial_field, plane_coupling, line_coupling, source, shift_table, shift_index):
    layer_count = initial_field.shape[0]
    layer_index = lax.broadcasted_iota(jnp.int32, initial_field.shape, 0)
    current = initial_field
    for half_step in range(HALF):
        shift_value = lookup(shift_table, shift_index[half_step])
        padded = padded_2(current, (("gx", 1), ("gy", 2)), 1)
        beside_all = (
            padded[:, 2:, 1:-1] + padded[:, :-2, 1:-1] + padded[:, 1:-1, 2:] + padded[:, 1:-1, :-2]
        )
        explicit = current + shift_value * (plane_coupling * (beside_all - 4.0 * current) + source)
        scaled = shift_value * line_coupling
        zero_field = jnp.zeros_like(scaled)
        forcing = jnp.stack(
            [
                explicit,
                jnp.where(layer_index == 0, scaled, zero_field),
                jnp.where(layer_index == layer_count - 1, scaled, zero_field),
            ]
        )
        solved = local_solve(scaled, forcing)
        interior = solved[0]
        from_left = solved[1]
        from_right = solved[2]
        left_value, right_value = reduced_gathered(
            interior[0], interior[-1], from_left[0], from_left[-1], from_right[0], from_right[-1]
        )
        current = interior + left_value * from_left + right_value * from_right
    return current


def solution(mesh):
    in_specs = (
        P("gz", "gx", "gy"),
        P("gz", "gx", "gy"),
        P("gz", "gx", "gy"),
        P("gz", "gx", "gy"),
        P(),
        P(),
    )
    out_specs = P("gz", "gx", "gy")
    return jax.shard_map(
        on_device, mesh=mesh, in_specs=in_specs, out_specs=out_specs, check_vma=False
    )
```

profile of v0, /device:TPU:24, one launch (start us, length us, event | category | flops | bytes accessed | tf_op | source)
XLA Modules:
  0.0 167.4 jit_solution(2650618903797842976)
XLA Ops:
  1.2 4.9 %collective-permute-start.3 = (f32[64,8,1]{2,1,0:T(8,128)S(1)}, f32[64,8,1]{2,1,0:T(8,128)S(1)}, u32[]{:S(2)}, u32[]{:S(2)}) collective-permute-start(f32[64,8,1]{2,1,0:T(8,128)S(1)} %get-tuple-element.1556), channel_id=1, source_target_pairs={{0,1},{1,2},{2,3},{3,4},{4,5},{5,6},{6,7},{7,8},{8,9},{9,10},{10,1... | collective-permute-start | bytes 6152 | tf_op jit(solution)/shard_map/ppermute | solution.py:41
  6.2 1.3 collective-permute-start
  7.5 3.0 %collective-permute-start.1 = (f32[64,1,128]{2,1,0:T(1,128)S(1)}, f32[64,1,128]{2,1,0:T(1,128)S(1)}, u32[]{:S(2)}, u32[]{:S(2)}) collective-permute-start(f32[64,1,128]{2,1,0:T(1,128)S(1)} %get-tuple-element.1557), channel_id=1, source_target_pairs={{0,32},{1,33},{2,34},{3,35},{4,36},{5,37},{6,38},{7,39},{8,40},{9,... | collective-permute-start | bytes 98312 | tf_op jit(solution)/shard_map/ppermute | solution.py:41
  10.6 3.3 %collective-permute-start.2 = (f32[64,8,1]{2,1,0:T(8,128)S(1)}, f32[64,8,1]{2,1,0:T(8,128)S(1)}, u32[]{:S(2)}, u32[]{:S(2)}) collective-permute-start(f32[64,8,1]{2,1,0:T(8,128)S(1)} %get-tuple-element.1555), channel_id=1, source_target_pairs={{1,0},{2,1},{3,2},{4,3},{5,4},{6,5},{7,6},{8,7},{9,8},{10,9},{11,1... | collective-permute-start | bytes 6152 | tf_op jit(solution)/shard_map/ppermute | solution.py:42
  15.2 3.1 %fusion.100 = (f32[]{:T(128)}, f32[]{:T(128)}, f32[]{:T(128)}, f32[]{:T(128)}) fusion(f32[8]{0:T(128)S(1)} %copy-done.70, s32[]{:T(128)} %bitcast, s32[]{:T(128)} %bitcast.17, s32[]{:T(128)} %bitcast.51, s32[]{:T(128)} %bitcast.34), kind=kLoop, calls=%fused_computation.414 | loop fusion | flops 92 | bytes 64 | tf_op jit(solution)/shard_map/reduce_sum | solution.py:55
  19.1 3.8 %add_add_fusion = (f32[64,8,128]{2,1,0:T(8,128)S(1)}, f32[64,8,128]{2,1,0:T(8,128)S(1)}, f32[64,8,128]{2,1,0:T(8,128)S(1)}, f32[64,8,128]{2,1,0:T(8,128)}, f32[6...) fusion(f32[64,8,128]{2,1,0:T(8,128)S(1)} %get-tuple-element.144, ...), kind=kLoop, calls=%fused_computation.250 | loop fusion | flops 1769472 | bytes 6537360 | tf_op jit(solution)/shard_map/add | solution.py:91
  23.2 3.2 %add_add_fusion.1 = (f32[64,8,128]{2,1,0:T(8,128)S(1)}, f32[64,8,128]{2,1,0:T(8,128)S(1)}, f32[64,8,128]{2,1,0:T(8,128)S(1)}, f32[64,8,128]{2,1,0:T(8,128)}, f32...) fusion(f32[64,8,128]{2,1,0:T(8,128)S(1)} %get-tuple-element.142, ...), kind=kLoop, calls=%fused_computation.281 | loop fusion | flops 1376256 | bytes 8077324 | tf_op jit(solution)/shard_map/add | solution.py:91
  45.1 3.3 %all-to-all-start = ((f32[2,1,48,128]{3,2,1,0:T(8,128)}), f32[2,1,48,128]{3,2,1,0:T(8,128)S(1)}, u32[]{:S(2)}, u32[]{:S(2)}) async-start(f32[2,1,48,128]{3,2,1,0:T(8,128)} %broadcast_in_dim.193), calls=%async_computation | async-start | bytes 98304 | tf_op jit(solution)/shard_map/all_to_all | solution.py:17
  48.4 1.9 %pad_multiply_fusion = (f32[64,8,128]{2,1,0:T(8,128)}, f32[64,8,128]{2,1,0:T(8,128)}) fusion(f32[48,8,128]{2,1,0:T(8,128)} %get-tuple-element.1400, f32[48,8,128]{2,1,0:T(8,128)} %get-tuple-element.1404, f32[64,8,128]{2,1,0:T(8,128)S(1)} %get-tuple-element.1226), kind=kLoop, calls=%fused_computation.228 | loop fusion | flops 196608 | bytes 1179648 | tf_op jit(solution)/shard_map/mul | solution.py:94
  50.3 2.1 %all-to-all-done = f32[2,1,48,128]{3,2,1,0:T(8,128)S(1)} async-done(((f32[2,1,48,128]{3,2,1,0:T(8,128)}), f32[2,1,48,128]{3,2,1,0:T(8,128)S(1)}, u32[]{:S(2)}, u32[]{:S(2)}) %all-to-all-start) | async-done | bytes 49184 | tf_op jit(solution)/shard_map/all_to_all | solution.py:17
  53.0 4.0 %collective-permute-start.7 = (f32[64,8,1]{2,1,0:T(8,128)S(1)}, f32[64,8,1]{2,1,0:T(8,128)S(1)}, u32[]{:S(2)}, u32[]{:S(2)}) collective-permute-start(f32[64,8,1]{2,1,0:T(8,128)S(1)} %get-tuple-element.1522), channel_id=1, source_target_pairs={{0,1},{1,2},{2,3},{3,4},{4,5},{5,6},{6,7},{7,8},{8,9},{9,10},{10,1... | collective-permute-start | bytes 6152 | tf_op jit(solution)/shard_map/ppermute | solution.py:41
  57.0 1.3 collective-permute-start.4
  58.3 3.0 %collective-permute-start.5 = (f32[64,1,128]{2,1,0:T(1,128)S(1)}, f32[64,1,128]{2,1,0:T(1,128)S(1)}, u32[]{:S(2)}, u32[]{:S(2)}) collective-permute-start(f32[64,1,128]{2,1,0:T(1,128)S(1)} %get-tuple-element.1523), channel_id=1, source_target_pairs={{0,32},{1,33},{2,34},{3,35},{4,36},{5,37},{6,38},{7,39},{8,40},{9,... | collective-permute-start | bytes 98312 | tf_op jit(solution)/shard_map/ppermute | solution.py:41
  61.4 4.2 %collective-permute-start.6 = (f32[64,8,1]{2,1,0:T(8,128)S(1)}, f32[64,8,1]{2,1,0:T(8,128)S(1)}, u32[]{:S(2)}, u32[]{:S(2)}) collective-permute-start(f32[64,8,1]{2,1,0:T(8,128)S(1)} %get-tuple-element.1521), channel_id=1, source_target_pairs={{1,0},{2,1},{3,2},{4,3},{5,4},{6,5},{7,6},{8,7},{9,8},{10,9},{11,1... | collective-permute-start | bytes 6152 | tf_op jit(solution)/shard_map/ppermute | solution.py:42
  66.4 7.3 %collective-permute-done.6 = f32[64,8,1]{2,1,0:T(8,128)S(1)} collective-permute-done((f32[64,8,1]{2,1,0:T(8,128)S(1)}, f32[64,8,1]{2,1,0:T(8,128)S(1)}, u32[]{:S(2)}, u32[]{:S(2)}) %collective-permute-start.6) | collective-permute-done | bytes 2080 | tf_op jit(solution)/shard_map/ppermute | solution.py:42
  82.6 3.5 %all-to-all-start.1 = ((f32[2,1,48,128]{3,2,1,0:T(8,128)}), f32[2,1,48,128]{3,2,1,0:T(8,128)S(1)}, u32[]{:S(2)}, u32[]{:S(2)}) async-start(f32[2,1,48,128]{3,2,1,0:T(8,128)} %broadcast_in_dim.194), calls=%async_computation.1 | async-start | bytes 98304 | tf_op jit(solution)/shard_map/all_to_all | solution.py:17
  86.1 1.8 %pad_multiply_fusion.1 = (f32[64,8,128]{2,1,0:T(8,128)}, f32[64,8,128]{2,1,0:T(8,128)S(1)}) fusion(f32[48,8,128]{2,1,0:T(8,128)} %get-tuple-element.1402, f32[48,8,128]{2,1,0:T(8,128)} %get-tuple-element.1403, f32[64,8,128]{2,1,0:T(8,128)S(1)} %get-tuple-element.1224), kind=kLoop, calls=%fused_computation.231 | loop fusion | flops 196608 | bytes 1179648 | tf_op jit(solution)/shard_map/mul | solution.py:93
  87.9 2.1 %all-to-all-done.1 = f32[2,1,48,128]{3,2,1,0:T(8,128)S(1)} async-done(((f32[2,1,48,128]{3,2,1,0:T(8,128)}), f32[2,1,48,128]{3,2,1,0:T(8,128)S(1)}, u32[]{:S(2)}, u32[]{:S(2)}) %all-to-all-start.1) | async-done | bytes 49184 | tf_op jit(solution)/shard_map/all_to_all | solution.py:17
  90.5 8.3 %collective-permute-start.11 = (f32[64,8,1]{2,1,0:T(8,128)S(1)}, f32[64,8,1]{2,1,0:T(8,128)S(1)}, u32[]{:S(2)}, u32[]{:S(2)}) collective-permute-start(f32[64,8,1]{2,1,0:T(8,128)S(1)} %get-tuple-element.1488), channel_id=1, source_target_pairs={{0,1},{1,2},{2,3},{3,4},{4,5},{5,6},{6,7},{7,8},{8,9},{9,10},{10,1... | collective-permute-start | bytes 6152 | tf_op jit(solution)/shard_map/ppermute | solution.py:41
  98.8 1.3 collective-permute-start.8
  100.1 3.0 %collective-permute-start.9 = (f32[64,1,128]{2,1,0:T(1,128)S(1)}, f32[64,1,128]{2,1,0:T(1,128)S(1)}, u32[]{:S(2)}, u32[]{:S(2)}) collective-permute-start(f32[64,1,128]{2,1,0:T(1,128)S(1)} %get-tuple-element.1489), channel_id=1, source_target_pairs={{0,32},{1,33},{2,34},{3,35},{4,36},{5,37},{6,38},{7,39},{8,40},{9,... | collective-permute-start | bytes 98312 | tf_op jit(solution)/shard_map/ppermute | solution.py:41
  103.1 1.9 %collective-permute-start.10 = (f32[64,8,1]{2,1,0:T(8,128)S(1)}, f32[64,8,1]{2,1,0:T(8,128)S(1)}, u32[]{:S(2)}, u32[]{:S(2)}) collective-permute-start(f32[64,8,1]{2,1,0:T(8,128)S(1)} %get-tuple-element.1487), channel_id=1, source_target_pairs={{1,0},{2,1},{3,2},{4,3},{5,4},{6,5},{7,6},{8,7},{9,8},{10,9},{11,1... | collective-permute-start | bytes 6152 | tf_op jit(solution)/shard_map/ppermute | solution.py:42
  105.9 8.2 %collective-permute-done.10 = f32[64,8,1]{2,1,0:T(8,128)S(1)} collective-permute-done((f32[64,8,1]{2,1,0:T(8,128)S(1)}, f32[64,8,1]{2,1,0:T(8,128)S(1)}, u32[]{:S(2)}, u32[]{:S(2)}) %collective-permute-start.10) | collective-permute-done | bytes 2080 | tf_op jit(solution)/shard_map/ppermute | solution.py:42
  123.0 3.3 %all-to-all-start.2 = ((f32[2,1,48,128]{3,2,1,0:T(8,128)}), f32[2,1,48,128]{3,2,1,0:T(8,128)S(1)}, u32[]{:S(2)}, u32[]{:S(2)}) async-start(f32[2,1,48,128]{3,2,1,0:T(8,128)} %broadcast_in_dim.195), calls=%async_computation.2 | async-start | bytes 98304 | tf_op jit(solution)/shard_map/all_to_all | solution.py:17
  127.3 3.0 %all-to-all-done.2 = f32[2,1,48,128]{3,2,1,0:T(8,128)S(1)} async-done(((f32[2,1,48,128]{3,2,1,0:T(8,128)}), f32[2,1,48,128]{3,2,1,0:T(8,128)S(1)}, u32[]{:S(2)}, u32[]{:S(2)}) %all-to-all-start.2) | async-done | bytes 49184 | tf_op jit(solution)/shard_map/all_to_all | solution.py:17
  130.8 4.9 %collective-permute-start.15 = (f32[64,8,1]{2,1,0:T(8,128)S(1)}, f32[64,8,1]{2,1,0:T(8,128)S(1)}, u32[]{:S(2)}, u32[]{:S(2)}) collective-permute-start(f32[64,8,1]{2,1,0:T(8,128)S(1)} %get-tuple-element.1444), channel_id=1, source_target_pairs={{0,1},{1,2},{2,3},{3,4},{4,5},{5,6},{6,7},{7,8},{8,9},{9,10},{10,1... | collective-permute-start | bytes 6152 | tf_op jit(solution)/shard_map/ppermute | solution.py:41
  135.8 1.3 collective-permute-start.12
  137.1 3.0 %collective-permute-start.13 = (f32[64,1,128]{2,1,0:T(1,128)S(1)}, f32[64,1,128]{2,1,0:T(1,128)S(1)}, u32[]{:S(2)}, u32[]{:S(2)}) collective-permute-start(f32[64,1,128]{2,1,0:T(1,128)S(1)} %get-tuple-element.1445), channel_id=1, source_target_pairs={{0,32},{1,33},{2,34},{3,35},{4,36},{5,37},{6,38},{7,39},{8,40},{9,... | collective-permute-start | bytes 98312 | tf_op jit(solution)/shard_map/ppermute | solution.py:41
  140.1 3.3 %collective-permute-start.14 = (f32[64,8,1]{2,1,0:T(8,128)S(1)}, f32[64,8,1]{2,1,0:T(8,128)S(1)}, u32[]{:S(2)}, u32[]{:S(2)}) collective-permute-start(f32[64,8,1]{2,1,0:T(8,128)S(1)} %get-tuple-element.1443), channel_id=1, source_target_pairs={{1,0},{2,1},{3,2},{4,3},{5,4},{6,5},{7,6},{8,7},{9,8},{10,9},{11,1... | collective-permute-start | bytes 6152 | tf_op jit(solution)/shard_map/ppermute | solution.py:42
  143.5 7.6 %collective-permute-done.14 = f32[64,8,1]{2,1,0:T(8,128)S(1)} collective-permute-done((f32[64,8,1]{2,1,0:T(8,128)S(1)}, f32[64,8,1]{2,1,0:T(8,128)S(1)}, u32[]{:S(2)}, u32[]{:S(2)}) %collective-permute-start.14) | collective-permute-done | bytes 2080 | tf_op jit(solution)/shard_map/ppermute | solution.py:42
  159.0 3.3 %all-to-all-start.3 = ((f32[2,1,48,128]{3,2,1,0:T(8,128)}), f32[2,1,48,128]{3,2,1,0:T(8,128)S(1)}, u32[]{:S(2)}, u32[]{:S(2)}) async-start(f32[2,1,48,128]{3,2,1,0:T(8,128)} %broadcast_in_dim.196), calls=%async_computation.3 | async-start | bytes 98304 | tf_op jit(solution)/shard_map/all_to_all | solution.py:17
  162.3 4.0 %all-to-all-done.3 = f32[2,1,48,128]{3,2,1,0:T(8,128)S(1)} async-done(((f32[2,1,48,128]{3,2,1,0:T(8,128)}), f32[2,1,48,128]{3,2,1,0:T(8,128)S(1)}, u32[]{:S(2)}, u32[]{:S(2)}) %all-to-all-start.3) | async-done | bytes 49184 | tf_op jit(solution)/shard_map/all_to_all | solution.py:17
  (451 shorter events, 51.9 us)
Async XLA Ops:
  0.0 6.2 %copy-start.2 = (f32[64,8,128]{2,1,0:T(8,128)S(1)}, f32[64,8,128]{2,1,0:T(8,128)}, u32[]{:S(2)}) copy-start(f32[64,8,128]{2,1,0:T(8,128)} %param.22) | copy-start | bytes 786436
  0.0 18.3 %copy-start.3 = (f32[64,8,128]{2,1,0:T(8,128)S(1)}, f32[64,8,128]{2,1,0:T(8,128)}, u32[]{:S(2)}) copy-start(f32[64,8,128]{2,1,0:T(8,128)} %param.24) | copy-start | bytes 786436
  1.2 40.2 %collective-permute-start.3 = (f32[64,8,1]{2,1,0:T(8,128)S(1)}, f32[64,8,1]{2,1,0:T(8,128)S(1)}, u32[]{:S(2)}, u32[]{:S(2)}) collective-permute-start(f32[64,8,1]{2,1,0:T(8,128)S(1)} %get-tuple-element.1556), channel_id=1, source_target_pairs={{0,1},{1,2},{2,3},{3,4},{4,5},{5,6},{6,7},{7,8},{8,9},{9,10},{10,1... | collective-permute-start | bytes 6152 | tf_op jit(solution)/shard_map/ppermute | solution.py:41
  6.2 35.2 %collective-permute-start = (f32[64,1,128]{2,1,0:T(1,128)S(1)}, f32[64,1,128]{2,1,0:T(1,128)S(1)}, u32[]{:S(2)}, u32[]{:S(2)}) collective-permute-start(f32[64,1,128]{2,1,0:T(1,128)S(1)} %get-tuple-element.1558), channel_id=1, source_target_pairs={{32,0},{33,1},{34,2},{35,3},{36,4},{37,5},{38,6},{39,7},{40,8},{41... | collective-permute-start | bytes 98312 | tf_op jit(solution)/shard_map/ppermute | solution.py:42
  7.5 33.9 %collective-permute-start.1 = (f32[64,1,128]{2,1,0:T(1,128)S(1)}, f32[64,1,128]{2,1,0:T(1,128)S(1)}, u32[]{:S(2)}, u32[]{:S(2)}) collective-permute-start(f32[64,1,128]{2,1,0:T(1,128)S(1)} %get-tuple-element.1557), channel_id=1, source_target_pairs={{0,32},{1,33},{2,34},{3,35},{4,36},{5,37},{6,38},{7,39},{8,40},{9,... | collective-permute-start | bytes 98312 | tf_op jit(solution)/shard_map/ppermute | solution.py:41
  10.6 3.3 %copy-start.69 = (s32[4]{0:T(128)S(1)}, s32[4]{0:T(128)}, u32[]{:S(2)}) copy-start(s32[4]{0:T(128)} %param.27) | copy-start | bytes 52
  10.6 30.8 %collective-permute-start.2 = (f32[64,8,1]{2,1,0:T(8,128)S(1)}, f32[64,8,1]{2,1,0:T(8,128)S(1)}, u32[]{:S(2)}, u32[]{:S(2)}) collective-permute-start(f32[64,8,1]{2,1,0:T(8,128)S(1)} %get-tuple-element.1555), channel_id=1, source_target_pairs={{1,0},{2,1},{3,2},{4,3},{5,4},{6,5},{7,6},{8,7},{9,8},{10,9},{11,1... | collective-permute-start | bytes 6152 | tf_op jit(solution)/shard_map/ppermute | solution.py:42
  37.6 3.0 %copy-start.40 = (f32[64,8,128]{2,1,0:T(8,128)}, f32[64,8,128]{2,1,0:T(8,128)S(1)}, u32[]{:S(2)}) copy-start(f32[64,8,128]{2,1,0:T(8,128)S(1)} %get-tuple-element.1227) | copy-start | bytes 786436
  38.5 2.1 %copy-start.42 = (f32[64,8,128]{2,1,0:T(8,128)}, f32[64,8,128]{2,1,0:T(8,128)S(1)}, u32[]{:S(2)}) copy-start(f32[64,8,128]{2,1,0:T(8,128)S(1)} %get-tuple-element.1225) | copy-start | bytes 786436
  45.1 7.3 %all-to-all-start = ((f32[2,1,48,128]{3,2,1,0:T(8,128)}), f32[2,1,48,128]{3,2,1,0:T(8,128)S(1)}, u32[]{:S(2)}, u32[]{:S(2)}) async-start(f32[2,1,48,128]{3,2,1,0:T(8,128)} %broadcast_in_dim.193), calls=%async_computation | async-start | bytes 98304 | tf_op jit(solution)/shard_map/all_to_all | solution.py:17
  53.0 13.4 %collective-permute-start.7 = (f32[64,8,1]{2,1,0:T(8,128)S(1)}, f32[64,8,1]{2,1,0:T(8,128)S(1)}, u32[]{:S(2)}, u32[]{:S(2)}) collective-permute-start(f32[64,8,1]{2,1,0:T(8,128)S(1)} %get-tuple-element.1522), channel_id=1, source_target_pairs={{0,1},{1,2},{2,3},{3,4},{4,5},{5,6},{6,7},{7,8},{8,9},{9,10},{10,1... | collective-permute-start | bytes 6152 | tf_op jit(solution)/shard_map/ppermute | solution.py:41
  57.0 16.6 %collective-permute-start.4 = (f32[64,1,128]{2,1,0:T(1,128)S(1)}, f32[64,1,128]{2,1,0:T(1,128)S(1)}, u32[]{:S(2)}, u32[]{:S(2)}) collective-permute-start(f32[64,1,128]{2,1,0:T(1,128)S(1)} %get-tuple-element.1524), channel_id=1, source_target_pairs={{32,0},{33,1},{34,2},{35,3},{36,4},{37,5},{38,6},{39,7},{40,8},{41... | collective-permute-start | bytes 98312 | tf_op jit(solution)/shard_map/ppermute | solution.py:42
  58.3 15.3 %collective-permute-start.5 = (f32[64,1,128]{2,1,0:T(1,128)S(1)}, f32[64,1,128]{2,1,0:T(1,128)S(1)}, u32[]{:S(2)}, u32[]{:S(2)}) collective-permute-start(f32[64,1,128]{2,1,0:T(1,128)S(1)} %get-tuple-element.1523), channel_id=1, source_target_pairs={{0,32},{1,33},{2,34},{3,35},{4,36},{5,37},{6,38},{7,39},{8,40},{9,... | collective-permute-start | bytes 98312 | tf_op jit(solution)/shard_map/ppermute | solution.py:41
  61.4 12.3 %collective-permute-start.6 = (f32[64,8,1]{2,1,0:T(8,128)S(1)}, f32[64,8,1]{2,1,0:T(8,128)S(1)}, u32[]{:S(2)}, u32[]{:S(2)}) collective-permute-start(f32[64,8,1]{2,1,0:T(8,128)S(1)} %get-tuple-element.1521), channel_id=1, source_target_pairs={{1,0},{2,1},{3,2},{4,3},{5,4},{6,5},{7,6},{8,7},{9,8},{10,9},{11,1... | collective-permute-start | bytes 6152 | tf_op jit(solution)/shard_map/ppermute | solution.py:42
  66.4 8.3 %copy-start.14 = (f32[1,64,8,128]{3,2,1,0:T(8,128)S(1)}, f32[1,64,8,128]{3,2,1,0:T(8,128)}, u32[]{:S(2)}) copy-start(f32[1,64,8,128]{3,2,1,0:T(8,128)} %get-tuple-element.1431) | copy-start | bytes 786436
  66.4 8.3 %copy-start.15 = (f32[1,64,8,128]{3,2,1,0:T(8,128)S(1)}, f32[1,64,8,128]{3,2,1,0:T(8,128)}, u32[]{:S(2)}) copy-start(f32[1,64,8,128]{3,2,1,0:T(8,128)} %get-tuple-element.1435) | copy-start | bytes 786436
  82.6 7.3 %all-to-all-start.1 = ((f32[2,1,48,128]{3,2,1,0:T(8,128)}), f32[2,1,48,128]{3,2,1,0:T(8,128)S(1)}, u32[]{:S(2)}, u32[]{:S(2)}) async-start(f32[2,1,48,128]{3,2,1,0:T(8,128)} %broadcast_in_dim.194), calls=%async_computation.1 | async-start | bytes 98304 | tf_op jit(solution)/shard_map/all_to_all | solution.py:17
  87.8 17.2 %copy-start.38 = (f32[64,8,128]{2,1,0:T(8,128)}, f32[64,8,128]{2,1,0:T(8,128)S(1)}, u32[]{:S(2)}) copy-start(f32[64,8,128]{2,1,0:T(8,128)S(1)} %get-tuple-element.1221) | copy-start | bytes 786436
  90.3 14.8 %copy-start.28 = (f32[64,8,128]{2,1,0:T(8,128)S(1)}, f32[64,8,128]{2,1,0:T(8,128)}, u32[]{:S(2)}) copy-start(f32[64,8,128]{2,1,0:T(8,128)} %get-tuple-element.1223) | copy-start | bytes 786436
  90.3 14.8 %copy-start.67 = (f32[48,8,128]{2,1,0:T(8,128)S(1)}, f32[48,8,128]{2,1,0:T(8,128)}, u32[]{:S(2)}) copy-start(f32[48,8,128]{2,1,0:T(8,128)} %get-tuple-element.1399) | copy-start | bytes 589828
  90.3 14.8 %copy-start.68 = (f32[48,8,128]{2,1,0:T(8,128)S(1)}, f32[48,8,128]{2,1,0:T(8,128)}, u32[]{:S(2)}) copy-start(f32[48,8,128]{2,1,0:T(8,128)} %get-tuple-element.1401) | copy-start | bytes 589828
  90.5 15.4 %collective-permute-start.11 = (f32[64,8,1]{2,1,0:T(8,128)S(1)}, f32[64,8,1]{2,1,0:T(8,128)S(1)}, u32[]{:S(2)}, u32[]{:S(2)}) collective-permute-start(f32[64,8,1]{2,1,0:T(8,128)S(1)} %get-tuple-element.1488), channel_id=1, source_target_pairs={{0,1},{1,2},{2,3},{3,4},{4,5},{5,6},{6,7},{7,8},{8,9},{9,10},{10,1... | collective-permute-start | bytes 6152 | tf_op jit(solution)/shard_map/ppermute | solution.py:41
  98.8 15.3 %collective-permute-start.8 = (f32[64,1,128]{2,1,0:T(1,128)S(1)}, f32[64,1,128]{2,1,0:T(1,128)S(1)}, u32[]{:S(2)}, u32[]{:S(2)}) collective-permute-start(f32[64,1,128]{2,1,0:T(1,128)S(1)} %get-tuple-element.1490), channel_id=1, source_target_pairs={{32,0},{33,1},{34,2},{35,3},{36,4},{37,5},{38,6},{39,7},{40,8},{41... | collective-permute-start | bytes 98312 | tf_op jit(solution)/shard_map/ppermute | solution.py:42
  100.1 14.0 %collective-permute-start.9 = (f32[64,1,128]{2,1,0:T(1,128)S(1)}, f32[64,1,128]{2,1,0:T(1,128)S(1)}, u32[]{:S(2)}, u32[]{:S(2)}) collective-permute-start(f32[64,1,128]{2,1,0:T(1,128)S(1)} %get-tuple-element.1489), channel_id=1, source_target_pairs={{0,32},{1,33},{2,34},{3,35},{4,36},{5,37},{6,38},{7,39},{8,40},{9,... | collective-permute-start | bytes 98312 | tf_op jit(solution)/shard_map/ppermute | solution.py:41
  103.1 11.0 %collective-permute-start.10 = (f32[64,8,1]{2,1,0:T(8,128)S(1)}, f32[64,8,1]{2,1,0:T(8,128)S(1)}, u32[]{:S(2)}, u32[]{:S(2)}) collective-permute-start(f32[64,8,1]{2,1,0:T(8,128)S(1)} %get-tuple-element.1487), channel_id=1, source_target_pairs={{1,0},{2,1},{3,2},{4,3},{5,4},{6,5},{7,6},{8,7},{9,8},{10,9},{11,1... | collective-permute-start | bytes 6152 | tf_op jit(solution)/shard_map/ppermute | solution.py:42
  122.2 4.1 %copy-start.52 = (f32[64,8,128]{2,1,0:T(8,128)S(1)}, f32[64,8,128]{2,1,0:T(8,128)}, u32[]{:S(2)}) copy-start(f32[64,8,128]{2,1,0:T(8,128)} %multiply_add_fusion.21) | copy-start | bytes 786436
  123.0 7.3 %all-to-all-start.2 = ((f32[2,1,48,128]{3,2,1,0:T(8,128)}), f32[2,1,48,128]{3,2,1,0:T(8,128)S(1)}, u32[]{:S(2)}, u32[]{:S(2)}) async-start(f32[2,1,48,128]{3,2,1,0:T(8,128)} %broadcast_in_dim.195), calls=%async_computation.2 | async-start | bytes 98304 | tf_op jit(solution)/shard_map/all_to_all | solution.py:17
  130.8 12.7 %collective-permute-start.15 = (f32[64,8,1]{2,1,0:T(8,128)S(1)}, f32[64,8,1]{2,1,0:T(8,128)S(1)}, u32[]{:S(2)}, u32[]{:S(2)}) collective-permute-start(f32[64,8,1]{2,1,0:T(8,128)S(1)} %get-tuple-element.1444), channel_id=1, source_target_pairs={{0,1},{1,2},{2,3},{3,4},{4,5},{5,6},{6,7},{7,8},{8,9},{9,10},{10,1... | collective-permute-start | bytes 6152 | tf_op jit(solution)/shard_map/ppermute | solution.py:41
  135.8 15.3 %collective-permute-start.12 = (f32[64,1,128]{2,1,0:T(1,128)S(1)}, f32[64,1,128]{2,1,0:T(1,128)S(1)}, u32[]{:S(2)}, u32[]{:S(2)}) collective-permute-start(f32[64,1,128]{2,1,0:T(1,128)S(1)} %get-tuple-element.1446), channel_id=1, source_target_pairs={{32,0},{33,1},{34,2},{35,3},{36,4},{37,5},{38,6},{39,7},{40,8},{41... | collective-permute-start | bytes 98312 | tf_op jit(solution)/shard_map/ppermute | solution.py:42
  137.1 14.0 %collective-permute-start.13 = (f32[64,1,128]{2,1,0:T(1,128)S(1)}, f32[64,1,128]{2,1,0:T(1,128)S(1)}, u32[]{:S(2)}, u32[]{:S(2)}) collective-permute-start(f32[64,1,128]{2,1,0:T(1,128)S(1)} %get-tuple-element.1445), channel_id=1, source_target_pairs={{0,32},{1,33},{2,34},{3,35},{4,36},{5,37},{6,38},{7,39},{8,40},{9,... | collective-permute-start | bytes 98312 | tf_op jit(solution)/shard_map/ppermute | solution.py:41
  140.1 11.0 %collective-permute-start.14 = (f32[64,8,1]{2,1,0:T(8,128)S(1)}, f32[64,8,1]{2,1,0:T(8,128)S(1)}, u32[]{:S(2)}, u32[]{:S(2)}) collective-permute-start(f32[64,8,1]{2,1,0:T(8,128)S(1)} %get-tuple-element.1443), channel_id=1, source_target_pairs={{1,0},{2,1},{3,2},{4,3},{5,4},{6,5},{7,6},{8,7},{9,8},{10,9},{11,1... | collective-permute-start | bytes 6152 | tf_op jit(solution)/shard_map/ppermute | solution.py:42
  159.0 7.3 %all-to-all-start.3 = ((f32[2,1,48,128]{3,2,1,0:T(8,128)}), f32[2,1,48,128]{3,2,1,0:T(8,128)S(1)}, u32[]{:S(2)}, u32[]{:S(2)}) async-start(f32[2,1,48,128]{3,2,1,0:T(8,128)} %broadcast_in_dim.196), calls=%async_computation.3 | async-start | bytes 98304 | tf_op jit(solution)/shard_map/all_to_all | solution.py:17
  (59 other events, 53.0 us)
where the time goes:
time: 169 us; the launch traced here: 167 us
  starting transfers between devices  65.5 us (39%)
  local copies, waits for them, and re-layouts  35.3 us (21%)
  waiting for transfers between devices  34.2 us (20%)
  other arithmetic  29.5 us (17%)
  between operations  2.33 us (1%)
    ppermute x8, starting transfers between devices, padded_2(): lax.ppermute(last, axis, up)  34.3 us
    unnamed x162, local copies, waits for them, and re-layouts  23.9 us
    ppermute x8, waiting for transfers between devices, padded_2(): lax.ppermute(first, axis, [(b, a) for a, b in up])  23.1 us
    ppermute x8, starting transfers between devices, padded_2(): lax.ppermute(first, axis, [(b, a) for a, b in up])  17.9 us
    all_to_all x4, starting transfers between devices, copy_for_each(): return lax.all_to_all(copies, axis, split_axis=0, concat_axis=0, tiled=True)  13.3 us
    add x22, other arithmetic, local_solve(): main_band + left_factor * upper_before + right_factor * lower_after  11.1 us
    all_to_all x4, waiting for transfers between devices, copy_for_each(): return lax.all_to_all(copies, axis, split_axis=0, concat_axis=0, tiled=True)  11.1 us
    slice x60, local copies, waits for them, and re-layouts, from_below(): lax.slice_in_dim(values, 0, values.shape[which_axis] - stride, axis=which...  4.73 us
  transfers between devices with their start and end apart: 20, of which 7 were waited for; matrix products, arithmetic and copies ran while one was open for 15% of the time, Pallas kernels for 0%

commit v1 on v0

v1 whole, which is shorter than its diff:
```python
import functools

import jax
import jax.numpy as jnp
from jax import lax
from jax.experimental import pallas as pl
from jax.experimental.pallas import tpu as pltpu
from jax.sharding import PartitionSpec as P

HALF = 4
NJ = 64
MESH = pl.DeviceIdType.MESH
U, PC, SRC, LC = range(4)
LC_FILL = 4000.0


def kernel(
    ny,
    u_hbm, pc_hbm, lc_hbm, src_hbm, table, rows,
    out_ref,
    raw, fac, prv, quo, dsc, mid, gtx, grx, dtx, drx,
    own_pk, own_rx, halo_pk, halo_rx, est, efac, eprv, equo, eds, erx,
    load_sem, raw_sem, own_sem, halo_sem, g_sem, d_sem, e_sem,
):
    gz, gx, gy = lax.axis_index("gz"), lax.axis_index("gx"), lax.axis_index("gy")
    has_left, has_right = gy > 0, gy < ny - 1
    y_left, y_right = lax.rem(gy + ny - 1, ny), lax.rem(gy + 1, ny)
    lane = lax.broadcasted_iota(jnp.int32, (8, 128), 1)
    row = lax.broadcasted_iota(jnp.int32, (8, 128), 0)
    base = 64 * gx + 32 * gz
    ones = jnp.full((8, 128), 1.0, jnp.float32)
    zero = jnp.zeros((8, 128), jnp.float32)

    def zof(j):
        return jnp.where(gz == 0, j, NJ - 1 - j)

    def remote(src, dst, send, recv, dev):
        return pltpu.make_async_remote_copy(
            src_ref=src, dst_ref=dst, send_sem=send, recv_sem=recv, device_id=dev, device_id_type=MESH
        )

    def roll(v, amount, axis=1):
        return pltpu.roll(v, amount, axis)

    loads = [
        pltpu.make_async_copy(ref, raw.at[a, gx], load_sem.at[a])
        for a, ref in ((LC, lc_hbm), (U, u_hbm), (PC, pc_hbm), (SRC, src_hbm))
    ]
    for c in loads:
        c.start()
    barrier = pltpu.get_barrier_semaphore()

    def hello(dev):
        pl.semaphore_signal(barrier, inc=1, device_id=dev, device_id_type=MESH)

    hello((gz, 1 - gx, gy))
    hello((1 - gz, gx, gy))
    hello((1 - gz, 1 - gx, gy))

    @pl.when((gx == 0) & has_left)
    def _():
        for z in range(2):
            for x in range(2):
                hello((z, x, y_left))

    @pl.when((gx == 1) & has_right)
    def _():
        for z in range(2):
            for x in range(2):
                hello((z, x, y_right))

    for c in loads:
        c.wait()

    def pack(g, _):
        for a in range(4):
            own_l, own_r, hl, hr = [zero, zero], [zero, zero], zero, zero
            for i in range(32):
                v = raw[a, gx, zof(g * 32 + i)]
                h, jj = i // 16, i % 16
                at = (4 + 8 * jj) % 128
                m8 = ((lane - at) & 127) < 8
                own_l[h] = jnp.where(m8, roll(v, at), own_l[h])
                own_r[h] = jnp.where(m8, roll(v, (at - 120) % 128), own_r[h])
                at = (12 + 4 * i) % 128
                hl = jnp.where(((lane - at) & 127) < 4, roll(v, at) if at else v, hl)
                at = 4 * i
                hr = jnp.where(((lane - at) & 127) < 4, roll(v, (at - 124) % 128), hr)
            for h in range(2):
                own_pk[0, a, 2 * g + h] = roll(own_l[h], base)
                own_pk[1, a, 2 * g + h] = roll(own_r[h], base)
            halo_pk[0, a, g] = roll(hl, base)
            halo_pk[1, a, g] = roll(hr, base)
        return 0

    lax.fori_loop(0, 2, pack, 0)
    for a in range(4):
        for g in range(4):
            own_rx[gx, gz, a, g] = own_pk[gx, a, g]

    pl.semaphore_wait(barrier, 3 + 2 * has_left.astype(jnp.int32) + 2 * has_right.astype(jnp.int32))

    raw_cp = [
        remote(raw.at[a, gx], raw.at[a, gx], raw_sem.at[0, a], raw_sem.at[1, a], (gz, 1 - gx, gy))
        for a in (LC, U, PC, SRC)
    ]
    for c in raw_cp:
        c.start()
    def halo_l():
        return [
            remote(halo_pk.at[0], halo_rx.at[gx, gz], halo_sem.at[0, 0, z], halo_sem.at[1, gx, gz], (z, 1, y_left))
            for z in range(2)
        ]

    def halo_r():
        return [
            remote(halo_pk.at[1], halo_rx.at[gx, gz], halo_sem.at[0, 1, z], halo_sem.at[1, gx, gz], (z, 0, y_right))
            for z in range(2)
        ]

    @pl.when(has_left)
    def _():
        for c in halo_l():
            c.start()

    @pl.when(has_right)
    def _():
        for c in halo_r():
            c.start()

    own_cp = [
        remote(own_pk.at[1 - gx], own_rx.at[gx, gz], own_sem.at[0, 0, 0], own_sem.at[1, gx, gz], (gz, 1 - gx, gy)),
        remote(own_pk.at[0], own_rx.at[gx, gz], own_sem.at[0, 0, 1], own_sem.at[1, gx, gz], (1 - gz, 0, gy)),
        remote(own_pk.at[1], own_rx.at[gx, gz], own_sem.at[0, 1, 0], own_sem.at[1, gx, gz], (1 - gz, 1, gy)),
    ]
    for c in own_cp:
        c.start()

    inv = []
    for k in range(HALF):
        shift = jnp.float32(0.0)
        for i in range(table.shape[0]):
            shift = shift + jnp.where(rows[k] == i, table[i], 0.0)
        inv.append(1.0 / jnp.full((8, 128), shift, jnp.float32))

    def factors(load_lc, store):
        def block(b, carry):
            ps, ds, rs = carry
            ps, ds, rs = list(ps), list(ds), list(rs)
            for i in range(4):
                j = b * 4 + i
                t_line = 1.0 / load_lc(j)
                for k in range(HALF):
                    old, r_old = ps[k], rs[k]
                    ds[k] = ds[k] + (t_line * inv[k]) * old
                    ps[k] = old + ds[k]
                    rs[k] = 1.0 / ps[k]
                    store(k, j, t_line * old, old, r_old * rs[k])
            return tuple(ps), tuple(ds), tuple(rs)

        start = (ones,) * HALF
        return lax.fori_loop(0, NJ // 4, block, (start, start, start))

    def main_factors(t):
        def store(k, j, f, p, q):
            z = zof(j)
            fac[k, t, z] = f
            prv[k, t, z] = p
            quo[k, t, z] = q

        ps, ds, rs = factors(lambda j: raw[LC, t, zof(j)], store)
        for k in range(HALF):
            mid[0, k, t] = rs[k]
            gtx[k, t] = ds[k] * rs[k]

    main_factors(gx)
    for c in raw_cp:
        c.wait()
    main_factors(1 - gx)
    g_cp = remote(gtx, grx, g_sem.at[0], g_sem.at[1], (1 - gz, gx, gy))
    g_cp.start()

    def forward_main(k):
        def block(b, totals):
            totals = list(totals)
            for i in range(4):
                z = zof(b * 4 + i)
                us = [raw[U, 0, z], raw[U, 1, z]]
                down = [roll(u, 1, 0) for u in us]
                up = [roll(u, 7, 0) for u in us]
                low = [jnp.where(row == 0, 0.0, down[0]), jnp.where(row == 0, down[0], down[1])]
                high = [jnp.where(row == 7, up[1], up[0]), jnp.where(row == 7, 0.0, up[1])]
                for t in range(2):
                    beside = (low[t] + high[t]) + (roll(us[t], 1) + roll(us[t], 127))
                    e = inv[k] * us[t] + raw[PC, t, z] * (beside - 4.0 * us[t]) + raw[SRC, t, z]
                    totals[t] = totals[t] + fac[k, t, z] * e
                    dsc[t, z] = totals[t]
            return tuple(totals)

        totals = lax.fori_loop(0, NJ // 4, block, (zero, zero))
        for t in range(2):
            dtx[k, t] = totals[t] * mid[0, k, t]
        cp = remote(dtx.at[k], drx.at[k], d_sem.at[0, k], d_sem.at[1, k], (1 - gz, gx, gy))
        cp.start()
        return cp

    def backward_main(k):
        last = zof(NJ - 1)
        ys = []
        for t in range(2):
            y = (dtx[k, t] + (1.0 - gtx[k, t]) * drx[k, t]) * mid[1, k, t]
            raw[U, t, last] = prv[k, t, last] * y
            ys.append(y)

        def block(b, ys):
            ys = list(ys)
            for i in range(7):
                z = zof(NJ - 2 - (b * 7 + i))
                for t in range(2):
                    ys[t] = ys[t] + dsc[t, z] * quo[k, t, z]
                    raw[U, t, z] = prv[k, t, z] * ys[t]
            return tuple(ys)

        lax.fori_loop(0, 9, block, tuple(ys))

    quads = [(x, z) for x in range(2) for z in range(2)]
    fills = {U: 0.0, PC: 0.0, SRC: 0.0, LC: LC_FILL}

    def unpack_own():
        def block(g, _):
            for jj in range(16):
                masks = [((lane - (64 * x + 32 * z + 4 + 8 * jj)) & 127) < 8 for x, z in quads]
                for a in range(4):
                    v = jnp.full((8, 128), fills[a], jnp.float32)
                    for (x, z), m in zip(quads, masks):
                        v = jnp.where(m, own_rx[x, z, a, g], v)
                    est[a, g * 16 + jj] = roll(v, (-8 * jj) % 128) if jj else v
            return 0

        lax.fori_loop(0, 4, block, 0)

    def unpack_halo():
        shifted = lane - 12 * gx

        def block(g, _):
            for jj in range(32):
                masks = [((shifted - (64 * x + 32 * z + 4 * jj)) & 127) < 4 for x, z in quads]
                m_all = (shifted & 31) < 4
                for a in range(4):
                    v = zero
                    for (x, z), m in zip(quads, masks):
                        v = jnp.where(m, halo_rx[x, z, a, g], v)
                    v = roll(v, (-4 * jj) % 128) if jj else v
                    est[a, g * 32 + jj] = jnp.where(m_all, v, est[a, g * 32 + jj])
            return 0

        lax.fori_loop(0, 2, block, 0)

    def edge_factors():
        def store(k, j, f, p, q):
            efac[k, j] = f
            eprv[k, j] = p
            equo[k, j] = q

        return factors(lambda j: est[LC, j], store)

    def other_half(v):
        return jnp.where((lane & 32) == 0, roll(v, 96), roll(v, 32))

    def edge_step(k, delta, recip):
        outer_low = (row == 0) & (lane < 64)
        outer_high = (row == 7) & (lane >= 64)

        def fwd(b, total):
            for i in range(4):
                j = b * 4 + i
                u = est[U, j]
                cross = roll(u, 64)
                low = jnp.where(outer_low, 0.0, roll(jnp.where(row == 7, cross, u), 1, 0))
                high = jnp.where(outer_high, 0.0, roll(jnp.where(row == 0, cross, u), 7, 0))
                beside = (low + high) + (roll(u, 1) + roll(u, 127))
                e = inv[k] * u + est[PC, j] * (beside - 4.0 * u) + est[SRC, j]
                total = total + efac[k, j] * e
                eds[j] = total
            return total

        total = lax.fori_loop(0, NJ // 4, fwd, zero)
        d = total * recip
        g = delta * recip
        last_p = eprv[k, NJ - 1]
        y = (d + (1.0 - g) * other_half(d)) / ((g + other_half(g) * (1.0 - g)) * last_p)
        est[U, NJ - 1] = last_p * y

        def back(b, y):
            for i in range(7):
                j = NJ - 2 - (b * 7 + i)
                y = y + eds[j] * equo[k, j]
                est[U, j] = eprv[k, j] * y
            return y

        lax.fori_loop(0, 9, back, y)

    cp = forward_main(0)
    for c in own_cp:
        c.wait_send()
    for x, z in quads:

        @pl.when((x != gx) | (z != gz))
        def _():
            remote(own_rx.at[x, z], own_rx.at[x, z], own_sem.at[0, 0, 0], own_sem.at[1, x, z], (gz, 1 - gx, gy)).wait_recv()

    unpack_own()
    g_cp.wait()
    for k in range(HALF):
        for t in range(2):
            g = gtx[k, t]
            mid[1, k, t] = 1.0 / ((g + grx[k, t] * (1.0 - g)) * prv[k, t, zof(NJ - 1)])
    cp.wait()
    backward_main(0)
    cp = forward_main(1)
    cp.wait()
    backward_main(1)
    cp = forward_main(2)

    @pl.when(has_left)
    def _():
        for c in halo_l():
            c.wait_send()

    @pl.when(has_right)
    def _():
        for c in halo_r():
            c.wait_send()

    @pl.when(((gx == 0) & has_left) | ((gx == 1) & has_right))
    def _():
        for x, z in quads:
            remote(halo_rx.at[x, z], halo_rx.at[x, z], halo_sem.at[0, 0, 0], halo_sem.at[1, x, z], (gz, 1 - gx, gy)).wait_recv()
        unpack_halo()

    e_ps, e_ds, e_rs = edge_factors()
    cp.wait()
    backward_main(2)
    cp = forward_main(3)
    for k in range(HALF):
        edge_step(k, e_ds[k], e_rs[k])
    e_cp = remote(est.at[U], erx, e_sem.at[0], e_sem.at[1], (gz, 1 - gx, gy))
    e_cp.start()
    cp.wait()
    backward_main(3)
    e_cp.wait()

    def shift_of(side):
        return (120 * side - (base + 4 + 4 * side) + 4 * side + 256) % 128

    mine, other = shift_of(gx), shift_of(1 - gx)
    first, last = lane < 4, lane >= 124
    mine_mask = (first & (gx == 0)) | (last & (gx == 1))
    other_mask = (first & (gx == 1)) | (last & (gx == 0))

    def merge(b, _):
        for i in range(8):
            j = b * 8 + i
            z = zof(j)
            v = jnp.where(mine_mask, roll(est[U, j], mine), raw[U, gx, z])
            out_ref[z] = jnp.where(other_mask, roll(erx[j], other), v)
        return 0

    lax.fori_loop(0, NJ // 8, merge, 0)


def solution(mesh):
    ny = mesh.shape["gy"]
    block = (NJ, 8, 128)
    vmem = lambda *s: pltpu.VMEM((*s, 8, 128), jnp.float32)

    def on_device(u, pc, lc, src, table, rows):
        hbm = pl.BlockSpec(memory_space=pl.ANY)
        smem = pl.BlockSpec(memory_space=pltpu.SMEM)
        return pl.pallas_call(
            functools.partial(kernel, ny),
            out_shape=jax.ShapeDtypeStruct(block, jnp.float32),
            in_specs=[hbm, hbm, hbm, hbm, smem, smem],
            out_specs=pl.BlockSpec(memory_space=pltpu.VMEM),
            scratch_shapes=[
                vmem(4, 2, NJ),
                vmem(HALF, 2, NJ), vmem(HALF, 2, NJ), vmem(HALF, 2, NJ),
                vmem(2, NJ), vmem(2, HALF, 2),
                vmem(HALF, 2), vmem(HALF, 2), vmem(HALF, 2), vmem(HALF, 2),
                vmem(2, 4, 4), vmem(2, 2, 4, 4), vmem(2, 4, 2), vmem(2, 2, 4, 2),
                vmem(4, NJ), vmem(HALF, NJ), vmem(HALF, NJ), vmem(HALF, NJ),
                vmem(NJ), vmem(NJ),
                pltpu.SemaphoreType.DMA((4,)),
                pltpu.SemaphoreType.DMA((2, 4)),
                pltpu.SemaphoreType.DMA((2, 2, 2)),
                pltpu.SemaphoreType.DMA((2, 2, 2)),
                pltpu.SemaphoreType.DMA((2,)),
                pltpu.SemaphoreType.DMA((2, HALF)),
                pltpu.SemaphoreType.DMA((2,)),
            ],
            compiler_params=pltpu.CompilerParams(collective_id=0, has_side_effects=True),
        )(u, pc, lc, src, table, rows)

    split = P("gz", "gx", "gy")
    return jax.shard_map(
        on_device, mesh=mesh, in_specs=(split,) * 4 + (P(), P()), out_specs=split, check_vma=False
    )
```

time: 169 us -> 34.6 us (0.20)
  the two profiles are of different devices: /device:TPU:24 before, /device:TPU:97 now
where the time goes in v1:
time: 34.6 us; the launch traced here: 34.4 us
  Pallas kernels  32.8 us (95%)
  local copies, waits for them, and re-layouts  1.67 us (5%)
    pallas_call x1, Pallas kernels, on_device(): pl.pallas_call(functools.partial(kernel, ny), out_shape=jax.ShapeDtypeStr...  32.8 us
    unnamed x1, local copies, waits for them, and re-layouts  1.67 us

profile of v1, /device:TPU:97, one launch (start us, length us, event | category | flops | bytes accessed | tf_op | source)
XLA Modules:
  0.0 34.4 jit_solution(11830178817979567738)
XLA Ops:
  0.0 32.8 %shard_map.64 = f32[64,8,128]{2,1,0:T(8,128)} custom-call(f32[64,8,128]{2,1,0:T(8,128)} %u_hbm.1, f32[64,8,128]{2,1,0:T(8,128)} %pc_hbm.1, f32[64,8,128]{2,1,0:T(8,128)} %lc_hbm.1, f32[64,8,128]{2,1,0:T(8,128)} %src_hbm.1, f32[8]{0:T(128)} %table.1, s32[4]{0:T(128)} %rows.1), custom_call_target="tpu_custom_call" | custom-call | tf_op jit(solution)/shard_map/pallas_call | solution.py:380
  32.8 1.7 %copy.8 = f32[64,8,128]{2,1,0:T(8,128)} copy(f32[64,8,128]{2,1,0:T(8,128)} %shard_map.64) | data formatting | bytes 524288

commit v2 on v1

--- a/solution.py
+++ b/solution.py
@@ -72,69 +72,37 @@
     for c in loads:
         c.wait()
 
+    low_half, even = (lane & 7) < 4, (lane & 8) == 0
+
     def pack(g, _):
         for a in range(4):
-            own_l, own_r, hl, hr = [zero, zero], [zero, zero], zero, zero
-            for i in range(32):
-                v = raw[a, gx, zof(g * 32 + i)]
-                h, jj = i // 16, i % 16
-                at = (4 + 8 * jj) % 128
-                m8 = ((lane - at) & 127) < 8
-                own_l[h] = jnp.where(m8, roll(v, at), own_l[h])
-                own_r[h] = jnp.where(m8, roll(v, (at - 120) % 128), own_r[h])
-                at = (12 + 4 * i) % 128
-                hl = jnp.where(((lane - at) & 127) < 4, roll(v, at) if at else v, hl)
-                at = 4 * i
-                hr = jnp.where(((lane - at) & 127) < 4, roll(v, (at - 124) % 128), hr)
+            left, right = [], []
             for h in range(2):
-                own_pk[0, a, 2 * g + h] = roll(own_l[h], base)
-                own_pk[1, a, 2 * g + h] = roll(own_r[h], base)
-            halo_pk[0, a, g] = roll(hl, base)
-            halo_pk[1, a, g] = roll(hr, base)
+                both = []
+                for q in range(2):
+                    v = zero
+                    for b in range(8):
+                        at = 16 * b
+                        w = roll(raw[a, gx, zof(g * 32 + h * 16 + q * 8 + b)], (at + 8) % 128)
+                        v = w if b == 0 else jnp.where((lane >= at) & (lane < at + 16), w, v)
+                    both.append(v)
+                left.append(jnp.where(even, roll(both[0], 120), both[1]))
+                right.append(jnp.where(even, both[0], roll(both[1], 8)))
+            for h in range(2):
+                own_pk[0, a, 2 * g + h] = roll(left[h], base + 4)
+                own_pk[1, a, 2 * g + h] = roll(right[h], base + 4)
+            halo_pk[0, a, g] = roll(jnp.where(low_half, left[0], roll(left[1], 4)), base + 12)
+            halo_pk[1, a, g] = roll(jnp.where(low_half, roll(right[0], 124), right[1]), base)
         return 0
 
-    lax.fori_loop(0, 2, pack, 0)
+    def octet(jj):
+        return 8 * (2 * jj if jj < 8 else 2 * (jj - 8) + 1)
+
+    with jax.named_scope("pack"):
+        lax.fori_loop(0, 2, pack, 0)
     for a in range(4):
         for g in range(4):
             own_rx[gx, gz, a, g] = own_pk[gx, a, g]
-
-    pl.semaphore_wait(barrier, 3 + 2 * has_left.astype(jnp.int32) + 2 * has_right.astype(jnp.int32))
-
-    raw_cp = [
-        remote(raw.at[a, gx], raw.at[a, gx], raw_sem.at[0, a], raw_sem.at[1, a], (gz, 1 - gx, gy))
-        for a in (LC, U, PC, SRC)
-    ]
-    for c in raw_cp:
-        c.start()
-    def halo_l():
-        return [
-            remote(halo_pk.at[0], halo_rx.at[gx, gz], halo_sem.at[0, 0, z], halo_sem.at[1, gx, gz], (z, 1, y_left))
-            for z in range(2)
-        ]
-
-    def halo_r():
-        return [
-            remote(halo_pk.at[1], halo_rx.at[gx, gz], halo_sem.at[0, 1, z], halo_sem.at[1, gx, gz], (z, 0, y_right))
-            for z in range(2)
-        ]
-
-    @pl.when(has_left)
-    def _():
-        for c in halo_l():
-            c.start()
-
-    @pl.when(has_right)
-    def _():
-        for c in halo_r():
-            c.start()
-
-    own_cp = [
-        remote(own_pk.at[1 - gx], own_rx.at[gx, gz], own_sem.at[0, 0, 0], own_sem.at[1, gx, gz], (gz, 1 - gx, gy)),
-        remote(own_pk.at[0], own_rx.at[gx, gz], own_sem.at[0, 0, 1], own_sem.at[1, gx, gz], (1 - gz, 0, gy)),
-        remote(own_pk.at[1], own_rx.at[gx, gz], own_sem.at[0, 1, 0], own_sem.at[1, gx, gz], (1 - gz, 1, gy)),
-    ]
-    for c in own_cp:
-        c.start()
 
     inv = []
     for k in range(HALF):
@@ -173,18 +141,61 @@
             mid[0, k, t] = rs[k]
             gtx[k, t] = ds[k] * rs[k]
 
-    main_factors(gx)
+    with jax.named_scope("fac0"):
+        main_factors(gx)
+
+    with jax.named_scope("wait_barrier"):
+        pl.semaphore_wait(barrier, 3 + 2 * has_left.astype(jnp.int32) + 2 * has_right.astype(jnp.int32))
+
+    raw_cp = [
+        remote(raw.at[a, gx], raw.at[a, gx], raw_sem.at[0, a], raw_sem.at[1, a], (gz, 1 - gx, gy))
+        for a in (LC, U, PC, SRC)
+    ]
     for c in raw_cp:
-        c.wait()
-    main_factors(1 - gx)
+        c.start()
+    def halo_l():
+        return [
+            remote(halo_pk.at[0], halo_rx.at[gx, gz], halo_sem.at[0, 0, z], halo_sem.at[1, gx, gz], (z, 1, y_left))
+            for z in range(2)
+        ]
+
+    def halo_r():
+        return [
+            remote(halo_pk.at[1], halo_rx.at[gx, gz], halo_sem.at[0, 1, z], halo_sem.at[1, gx, gz], (z, 0, y_right))
+            for z in range(2)
+        ]
+
+    @pl.when(has_left)
+    def _():
+        for c in halo_l():
+            c.start()
+
+    @pl.when(has_right)
+    def _():
+        for c in halo_r():
+            c.start()
+
+    own_cp = [
+        remote(own_pk.at[1 - gx], own_rx.at[gx, gz], own_sem.at[0, 0, 0], own_sem.at[1, gx, gz], (gz, 1 - gx, gy)),
+        remote(own_pk.at[0], own_rx.at[gx, gz], own_sem.at[0, 0, 1], own_sem.at[1, gx, gz], (1 - gz, 0, gy)),
+        remote(own_pk.at[1], own_rx.at[gx, gz], own_sem.at[0, 1, 0], own_sem.at[1, gx, gz], (1 - gz, 1, gy)),
+    ]
+    for c in own_cp:
+        c.start()
+
+    with jax.named_scope("wait_raw"):
+        for c in raw_cp:
+            c.wait()
+    with jax.named_scope("fac1"):
+        main_factors(1 - gx)
     g_cp = remote(gtx, grx, g_sem.at[0], g_sem.at[1], (1 - gz, gx, gy))
     g_cp.start()
 
     def forward_main(k):
         def block(b, totals):
             totals = list(totals)
-            for i in range(4):
-                z = zof(b * 4 + i)
+            for i in range(16):
+                z = zof(b * 16 + i)
                 us = [raw[U, 0, z], raw[U, 1, z]]
                 down = [roll(u, 1, 0) for u in us]
                 up = [roll(u, 7, 0) for u in us]
@@ -197,7 +208,7 @@
                     dsc[t, z] = totals[t]
             return tuple(totals)
 
-        totals = lax.fori_loop(0, NJ // 4, block, (zero, zero))
+        totals = lax.fori_loop(0, NJ // 16, block, (zero, zero))
         for t in range(2):
             dtx[k, t] = totals[t] * mid[0, k, t]
         cp = remote(dtx.at[k], drx.at[k], d_sem.at[0, k], d_sem.at[1, k], (1 - gz, gx, gy))
@@ -229,12 +240,12 @@
     def unpack_own():
         def block(g, _):
             for jj in range(16):
-                masks = [((lane - (64 * x + 32 * z + 4 + 8 * jj)) & 127) < 8 for x, z in quads]
+                masks = [((lane - (64 * x + 32 * z + 4 + octet(jj))) & 127) < 8 for x, z in quads]
                 for a in range(4):
                     v = jnp.full((8, 128), fills[a], jnp.float32)
                     for (x, z), m in zip(quads, masks):
                         v = jnp.where(m, own_rx[x, z, a, g], v)
-                    est[a, g * 16 + jj] = roll(v, (-8 * jj) % 128) if jj else v
+                    est[a, g * 16 + jj] = roll(v, (-octet(jj)) % 128) if jj else v
             return 0
 
         lax.fori_loop(0, 4, block, 0)
@@ -244,13 +255,14 @@
 
         def block(g, _):
             for jj in range(32):
-                masks = [((shifted - (64 * x + 32 * z + 4 * jj)) & 127) < 4 for x, z in quads]
+                at = octet(jj) if jj < 16 else octet(jj - 16) + 4
+                masks = [((shifted - (64 * x + 32 * z + at)) & 127) < 4 for x, z in quads]
                 m_all = (shifted & 31) < 4
                 for a in range(4):
                     v = zero
                     for (x, z), m in zip(quads, masks):
                         v = jnp.where(m, halo_rx[x, z, a, g], v)
-                    v = roll(v, (-4 * jj) % 128) if jj else v
+                    v = roll(v, (-at) % 128) if at else v
                     est[a, g * 32 + jj] = jnp.where(m_all, v, est[a, g * 32 + jj])
             return 0
 
@@ -272,8 +284,8 @@
         outer_high = (row == 7) & (lane >= 64)
 
         def fwd(b, total):
-            for i in range(4):
-                j = b * 4 + i
+            for i in range(16):
+                j = b * 16 + i
                 u = est[U, j]
                 cross = roll(u, 64)
                 low = jnp.where(outer_low, 0.0, roll(jnp.where(row == 7, cross, u), 1, 0))
@@ -284,7 +296,7 @@
                 eds[j] = total
             return total
 
-        total = lax.fori_loop(0, NJ // 4, fwd, zero)
+        total = lax.fori_loop(0, NJ // 16, fwd, zero)
         d = total * recip
         g = delta * recip
         last_p = eprv[k, NJ - 1]
@@ -300,7 +312,8 @@
 
         lax.fori_loop(0, 9, back, y)
 
-    cp = forward_main(0)
+    with jax.named_scope("f0"):
+        cp = forward_main(0)
     for c in own_cp:
         c.wait_send()
     for x, z in quads:
@@ -309,18 +322,26 @@
         def _():
             remote(own_rx.at[x, z], own_rx.at[x, z], own_sem.at[0, 0, 0], own_sem.at[1, x, z], (gz, 1 - gx, gy)).wait_recv()
 
-    unpack_own()
-    g_cp.wait()
+    with jax.named_scope("unpack_own"):
+        unpack_own()
+    with jax.named_scope("wait_g"):
+        g_cp.wait()
     for k in range(HALF):
         for t in range(2):
             g = gtx[k, t]
             mid[1, k, t] = 1.0 / ((g + grx[k, t] * (1.0 - g)) * prv[k, t, zof(NJ - 1)])
-    cp.wait()
-    backward_main(0)
-    cp = forward_main(1)
-    cp.wait()
-    backward_main(1)
-    cp = forward_main(2)
+    with jax.named_scope("w0"):
+        cp.wait()
+    with jax.named_scope("b0"):
+        backward_main(0)
+    with jax.named_scope("f1"):
+        cp = forward_main(1)
+    with jax.named_scope("w1"):
+        cp.wait()
+    with jax.named_scope("b1"):
+        backward_main(1)
+    with jax.named_scope("f2"):
+        cp = forward_main(2)
 
     @pl.when(has_left)
     def _():
@@ -336,19 +357,28 @@
     def _():
         for x, z in quads:
             remote(halo_rx.at[x, z], halo_rx.at[x, z], halo_sem.at[0, 0, 0], halo_sem.at[1, x, z], (gz, 1 - gx, gy)).wait_recv()
-        unpack_halo()
-
-    e_ps, e_ds, e_rs = edge_factors()
-    cp.wait()
-    backward_main(2)
-    cp = forward_main(3)
+        with jax.named_scope("unpack_halo"):
+            unpack_halo()
+
+    with jax.named_scope("edge_fac"):
+        e_ps, e_ds, e_rs = edge_factors()
+    with jax.named_scope("w2"):
+        cp.wait()
+    with jax.named_scope("b2"):
+        backward_main(2)
+    with jax.named_scope("f3"):
+        cp = forward_main(3)
     for k in range(HALF):
-        edge_step(k, e_ds[k], e_rs[k])
+        with jax.named_scope(f"e{k}"):
+            edge_step(k, e_ds[k], e_rs[k])
     e_cp = remote(est.at[U], erx, e_sem.at[0], e_sem.at[1], (gz, 1 - gx, gy))
     e_cp.start()
-    cp.wait()
-    backward_main(3)
-    e_cp.wait()
+    with jax.named_scope("w3"):
+        cp.wait()
+    with jax.named_scope("b3"):
+        backward_main(3)
+    with jax.named_scope("we"):
+        e_cp.wait()
 
     def shift_of(side):
         return (120 * side - (base + 4 + 4 * side) + 4 * side + 256) % 128
@@ -366,7 +396,8 @@
             out_ref[z] = jnp.where(other_mask, roll(erx[j], other), v)
         return 0
 
-    lax.fori_loop(0, NJ // 8, merge, 0)
+    with jax.named_scope("merge"):
+        lax.fori_loop(0, NJ // 8, merge, 0)
 
 
 def solution(mesh):

time: 34.6 us -> 28.2 us (0.82)
  Pallas kernels: 32.8 us -> 26.3 us
    pallas_call x1, Pallas kernels: 32.8 us -> 26.3 us  [on_device(): pl.pallas_call(functools.partial(kernel, ny), out_shape=jax.ShapeDtypeStr...]
where the time goes in v2:
time: 28.2 us; the launch traced here: 28 us
  Pallas kernels  26.3 us (93%)
  local copies, waits for them, and re-layouts  1.67 us (6%)
    pallas_call x1, Pallas kernels, on_device(): pl.pallas_call(functools.partial(kernel, ny), out_shape=jax.ShapeDtypeStr...  26.3 us
    unnamed x1, local copies, waits for them, and re-layouts  1.67 us

profile of v2, /device:TPU:97, one launch (start us, length us, event | category | flops | bytes accessed | tf_op | source)
XLA Modules:
  0.0 28.0 jit_solution(13480889497128429309)
XLA Ops:
  0.0 26.3 %shard_map.64 = f32[64,8,128]{2,1,0:T(8,128)} custom-call(f32[64,8,128]{2,1,0:T(8,128)} %u_hbm.1, f32[64,8,128]{2,1,0:T(8,128)} %pc_hbm.1, f32[64,8,128]{2,1,0:T(8,128)} %lc_hbm.1, f32[64,8,128]{2,1,0:T(8,128)} %src_hbm.1, f32[8]{0:T(128)} %table.1, s32[4]{0:T(128)} %rows.1), custom_call_target="tpu_custom_call" | custom-call | tf_op jit(solution)/shard_map/pallas_call | solution.py:411
  26.3 1.7 %copy.8 = f32[64,8,128]{2,1,0:T(8,128)} copy(f32[64,8,128]{2,1,0:T(8,128)} %shard_map.64) | data formatting | bytes 524288

commit v3 on v2

--- a/solution.py
+++ b/solution.py
@@ -16,11 +16,11 @@
 
 def kernel(
     ny,
-    u_hbm, pc_hbm, lc_hbm, src_hbm, table, rows,
+    u_hbm, pc_hbm, lc_hbm, src_hbm, table_hbm, rows_hbm,
     out_ref,
     raw, fac, prv, quo, dsc, mid, gtx, grx, dtx, drx,
     own_pk, own_rx, halo_pk, halo_rx, est, efac, eprv, equo, eds, erx,
-    load_sem, raw_sem, own_sem, halo_sem, g_sem, d_sem, e_sem,
+    table, rows, load_sem, raw_sem, own_sem, halo_sem, g_sem, d0_sem, d_sem, e_sem, go,
 ):
     gz, gx, gy = lax.axis_index("gz"), lax.axis_index("gx"), lax.axis_index("gy")
     has_left, has_right = gy > 0, gy < ny - 1
@@ -46,28 +46,30 @@
         pltpu.make_async_copy(ref, raw.at[a, gx], load_sem.at[a])
         for a, ref in ((LC, lc_hbm), (U, u_hbm), (PC, pc_hbm), (SRC, src_hbm))
     ]
+    loads.append(pltpu.make_async_copy(table_hbm, table, load_sem.at[4]))
+    loads.append(pltpu.make_async_copy(rows_hbm, rows, load_sem.at[5]))
     for c in loads:
         c.start()
     barrier = pltpu.get_barrier_semaphore()
 
-    def hello(dev):
-        pl.semaphore_signal(barrier, inc=1, device_id=dev, device_id_type=MESH)
-
-    hello((gz, 1 - gx, gy))
-    hello((1 - gz, gx, gy))
-    hello((1 - gz, 1 - gx, gy))
-
-    @pl.when((gx == 0) & has_left)
+    def hello(sem, dev):
+        pl.semaphore_signal(sem, inc=1, device_id=dev, device_id_type=MESH)
+
+    hello(barrier, (1 - gz, 1, gy))
+
+    @pl.when(gx == 0)
     def _():
-        for z in range(2):
-            for x in range(2):
-                hello((z, x, y_left))
+        hello(barrier, (gz, 1, gy))
+
+        @pl.when(has_left)
+        def _():
+            for z in range(2):
+                hello(barrier, (z, 0, y_left))
 
     @pl.when((gx == 1) & has_right)
     def _():
         for z in range(2):
-            for x in range(2):
-                hello((z, x, y_right))
+            hello(barrier, (z, 0, y_right))
 
     for c in loads:
         c.wait()
@@ -139,20 +141,35 @@
         ps, ds, rs = factors(lambda j: raw[LC, t, zof(j)], store)
         for k in range(HALF):
             mid[0, k, t] = rs[k]
-            gtx[k, t] = ds[k] * rs[k]
+            gtx[t, k] = ds[k] * rs[k]
 
     with jax.named_scope("fac0"):
         main_factors(gx)
 
     with jax.named_scope("wait_barrier"):
-        pl.semaphore_wait(barrier, 3 + 2 * has_left.astype(jnp.int32) + 2 * has_right.astype(jnp.int32))
-
-    raw_cp = [
-        remote(raw.at[a, gx], raw.at[a, gx], raw_sem.at[0, a], raw_sem.at[1, a], (gz, 1 - gx, gy))
-        for a in (LC, U, PC, SRC)
-    ]
-    for c in raw_cp:
+
+        @pl.when(gx == 1)
+        def _():
+            pl.semaphore_wait(barrier, 3)
+            hello(go, (gz, 0, gy))
+
+        @pl.when(gx == 0)
+        def _():
+            pl.semaphore_wait(go, 1)
+
+    raw_cp = {
+        a: remote(raw.at[a, gx], raw.at[a, gx], raw_sem.at[0, a], raw_sem.at[1, a], (gz, 1 - gx, gy))
+        for a in (U, LC, PC, SRC)
+    }
+    for c in raw_cp.values():
         c.start()
+
+    def g_copy(x):
+        return remote(gtx.at[gx], grx.at[gx], g_sem.at[0, x], g_sem.at[1, gx], (1 - gz, x, gy))
+
+    for x in (1, 0):
+        g_copy(x).start()
+
     def halo_l():
         return [
             remote(halo_pk.at[0], halo_rx.at[gx, gz], halo_sem.at[0, 0, z], halo_sem.at[1, gx, gz], (z, 1, y_left))
@@ -165,37 +182,63 @@
             for z in range(2)
         ]
 
-    @pl.when(has_left)
-    def _():
-        for c in halo_l():
-            c.start()
-
-    @pl.when(has_right)
-    def _():
-        for c in halo_r():
-            c.start()
-
     own_cp = [
         remote(own_pk.at[1 - gx], own_rx.at[gx, gz], own_sem.at[0, 0, 0], own_sem.at[1, gx, gz], (gz, 1 - gx, gy)),
         remote(own_pk.at[0], own_rx.at[gx, gz], own_sem.at[0, 0, 1], own_sem.at[1, gx, gz], (1 - gz, 0, gy)),
         remote(own_pk.at[1], own_rx.at[gx, gz], own_sem.at[0, 1, 0], own_sem.at[1, gx, gz], (1 - gz, 1, gy)),
     ]
-    for c in own_cp:
-        c.start()
-
-    with jax.named_scope("wait_raw"):
-        for c in raw_cp:
-            c.wait()
-    with jax.named_scope("fac1"):
-        main_factors(1 - gx)
-    g_cp = remote(gtx, grx, g_sem.at[0], g_sem.at[1], (1 - gz, gx, gy))
-    g_cp.start()
+
+    def start_halos():
+        @pl.when(gx == 0)
+        def _():
+            pl.semaphore_wait(barrier, 2 * has_left.astype(jnp.int32) + 2 * has_right.astype(jnp.int32))
+            hello(go, (gz, 1, gy))
+
+        @pl.when(gx == 1)
+        def _():
+            pl.semaphore_wait(go, 1)
+
+        @pl.when(has_left)
+        def _():
+            for c in halo_l():
+                c.start()
+
+        @pl.when(has_right)
+        def _():
+            for c in halo_r():
+                c.start()
+
+    def d0_copy(x):
+        return remote(dtx.at[0, gx], drx.at[0, gx], d0_sem.at[0, x], d0_sem.at[1, gx], (1 - gz, x, gy))
+
+    def d_copy(k, x):
+        return remote(dtx.at[k], drx.at[k], d_sem.at[x, k], d_sem.at[2, k], (1 - gz, x, gy))
+
+    def wait_d(k):
+        d_copy(k, 0).wait_recv()
+
+    low_on, high_on = gx.astype(jnp.float32), (1 - gx).astype(jnp.float32)
+
+    def forward_tile(t, low_on, high_on):
+        def block(b, total):
+            for i in range(32):
+                z = zof(b * 32 + i)
+                u, v = raw[U, t, z], raw[U, 1 - t, z]
+                low = jnp.where(row == 0, roll(v, 1, 0) * low_on, roll(u, 1, 0))
+                high = jnp.where(row == 7, roll(v, 7, 0) * high_on, roll(u, 7, 0))
+                beside = (low + high) + (roll(u, 1) + roll(u, 127))
+                e = inv[0] * u + raw[PC, t, z] * (beside - 4.0 * u) + raw[SRC, t, z]
+                total = total + fac[0, t, z] * e
+                dsc[t, z] = total
+            return total
+
+        dtx[0, t] = lax.fori_loop(0, NJ // 32, block, zero) * mid[0, 0, t]
 
     def forward_main(k):
         def block(b, totals):
             totals = list(totals)
-            for i in range(16):
-                z = zof(b * 16 + i)
+            for i in range(32):
+                z = zof(b * 32 + i)
                 us = [raw[U, 0, z], raw[U, 1, z]]
                 down = [roll(u, 1, 0) for u in us]
                 up = [roll(u, 7, 0) for u in us]
@@ -208,31 +251,32 @@
                     dsc[t, z] = totals[t]
             return tuple(totals)
 
-        totals = lax.fori_loop(0, NJ // 16, block, (zero, zero))
+        totals = lax.fori_loop(0, NJ // 32, block, (zero, zero))
         for t in range(2):
             dtx[k, t] = totals[t] * mid[0, k, t]
-        cp = remote(dtx.at[k], drx.at[k], d_sem.at[0, k], d_sem.at[1, k], (1 - gz, gx, gy))
-        cp.start()
-        return cp
+        @pl.when(gx == 1)
+        def _():
+            for x in (1, 0):
+                d_copy(k, x).start()
 
     def backward_main(k):
         last = zof(NJ - 1)
         ys = []
         for t in range(2):
-            y = (dtx[k, t] + (1.0 - gtx[k, t]) * drx[k, t]) * mid[1, k, t]
+            y = (dtx[k, t] + (1.0 - gtx[t, k]) * drx[k, t]) * mid[1, k, t]
             raw[U, t, last] = prv[k, t, last] * y
             ys.append(y)
 
         def block(b, ys):
             ys = list(ys)
-            for i in range(7):
-                z = zof(NJ - 2 - (b * 7 + i))
+            for i in range(21):
+                z = zof(NJ - 2 - (b * 21 + i))
                 for t in range(2):
                     ys[t] = ys[t] + dsc[t, z] * quo[k, t, z]
                     raw[U, t, z] = prv[k, t, z] * ys[t]
             return tuple(ys)
 
-        lax.fori_loop(0, 9, block, tuple(ys))
+        lax.fori_loop(0, 3, block, tuple(ys))
 
     quads = [(x, z) for x in range(2) for z in range(2)]
     fills = {U: 0.0, PC: 0.0, SRC: 0.0, LC: LC_FILL}
@@ -284,8 +328,8 @@
         outer_high = (row == 7) & (lane >= 64)
 
         def fwd(b, total):
-            for i in range(16):
-                j = b * 16 + i
+            for i in range(32):
+                j = b * 32 + i
                 u = est[U, j]
                 cross = roll(u, 64)
                 low = jnp.where(outer_low, 0.0, roll(jnp.where(row == 7, cross, u), 1, 0))
@@ -296,7 +340,7 @@
                 eds[j] = total
             return total
 
-        total = lax.fori_loop(0, NJ // 16, fwd, zero)
+        total = lax.fori_loop(0, NJ // 32, fwd, zero)
         d = total * recip
         g = delta * recip
         last_p = eprv[k, NJ - 1]
@@ -304,45 +348,61 @@
         est[U, NJ - 1] = last_p * y
 
         def back(b, y):
-            for i in range(7):
-                j = NJ - 2 - (b * 7 + i)
+            for i in range(21):
+                j = NJ - 2 - (b * 21 + i)
                 y = y + eds[j] * equo[k, j]
                 est[U, j] = eprv[k, j] * y
             return y
 
-        lax.fori_loop(0, 9, back, y)
-
+        lax.fori_loop(0, 3, back, y)
+
+    with jax.named_scope("wait_y"):
+        start_halos()
+    for c in own_cp:
+        c.start()
+
+    with jax.named_scope("wait_u"):
+        raw_cp[U].wait()
     with jax.named_scope("f0"):
-        cp = forward_main(0)
-    for c in own_cp:
-        c.wait_send()
-    for x, z in quads:
-
-        @pl.when((x != gx) | (z != gz))
-        def _():
-            remote(own_rx.at[x, z], own_rx.at[x, z], own_sem.at[0, 0, 0], own_sem.at[1, x, z], (gz, 1 - gx, gy)).wait_recv()
-
-    with jax.named_scope("unpack_own"):
-        unpack_own()
+        forward_tile(gx, low_on, high_on)
+        for x in (1, 0):
+            d0_copy(x).start()
+    with jax.named_scope("wait_raw"):
+        for a in (LC, PC, SRC):
+            raw_cp[a].wait()
+    with jax.named_scope("fac1"):
+        main_factors(1 - gx)
+    with jax.named_scope("f0b"):
+        forward_tile(1 - gx, high_on, low_on)
     with jax.named_scope("wait_g"):
-        g_cp.wait()
+        for x in range(2):
+            g_copy(x).wait_send()
+        for t in range(2):
+            remote(gtx.at[t], grx.at[t], g_sem.at[0, 0], g_sem.at[1, t], (1 - gz, 0, gy)).wait_recv()
     for k in range(HALF):
         for t in range(2):
-            g = gtx[k, t]
-            mid[1, k, t] = 1.0 / ((g + grx[k, t] * (1.0 - g)) * prv[k, t, zof(NJ - 1)])
+            g = gtx[t, k]
+            mid[1, k, t] = 1.0 / ((g + grx[t, k] * (1.0 - g)) * prv[k, t, zof(NJ - 1)])
     with jax.named_scope("w0"):
-        cp.wait()
+        for x in range(2):
+            d0_copy(x).wait_send()
+        for t in range(2):
+            remote(dtx.at[0, t], drx.at[0, t], d0_sem.at[0, 0], d0_sem.at[1, t], (1 - gz, 0, gy)).wait_recv()
     with jax.named_scope("b0"):
         backward_main(0)
     with jax.named_scope("f1"):
-        cp = forward_main(1)
-    with jax.named_scope("w1"):
-        cp.wait()
-    with jax.named_scope("b1"):
-        backward_main(1)
-    with jax.named_scope("f2"):
-        cp = forward_main(2)
-
+        forward_main(1)
+    with jax.named_scope("wait_own"):
+        for c in own_cp:
+            c.wait_send()
+        for x, z in quads:
+
+            @pl.when((x != gx) | (z != gz))
+            def _():
+                remote(own_rx.at[x, z], own_rx.at[x, z], own_sem.at[0, 0, 0], own_sem.at[1, x, z], (gz, 1 - gx, gy)).wait_recv()
+
+    with jax.named_scope("unpack_own"):
+        unpack_own()
     @pl.when(has_left)
     def _():
         for c in halo_l():
@@ -355,6 +415,7 @@
 
     @pl.when(((gx == 0) & has_left) | ((gx == 1) & has_right))
     def _():
+      with jax.named_scope("wait_halo"):
         for x, z in quads:
             remote(halo_rx.at[x, z], halo_rx.at[x, z], halo_sem.at[0, 0, 0], halo_sem.at[1, x, z], (gz, 1 - gx, gy)).wait_recv()
         with jax.named_scope("unpack_halo"):
@@ -362,24 +423,40 @@
 
     with jax.named_scope("edge_fac"):
         e_ps, e_ds, e_rs = edge_factors()
+    with jax.named_scope("w1"):
+        wait_d(1)
+    with jax.named_scope("b1"):
+        backward_main(1)
+    with jax.named_scope("f2"):
+        forward_main(2)
+
+    for k in range(3):
+        with jax.named_scope(f"e{k}"):
+            edge_step(k, e_ds[k], e_rs[k])
     with jax.named_scope("w2"):
-        cp.wait()
+        wait_d(2)
     with jax.named_scope("b2"):
         backward_main(2)
     with jax.named_scope("f3"):
-        cp = forward_main(3)
-    for k in range(HALF):
+        forward_main(3)
+    for k in range(3, HALF):
         with jax.named_scope(f"e{k}"):
             edge_step(k, e_ds[k], e_rs[k])
     e_cp = remote(est.at[U], erx, e_sem.at[0], e_sem.at[1], (gz, 1 - gx, gy))
     e_cp.start()
     with jax.named_scope("w3"):
-        cp.wait()
+        wait_d(3)
     with jax.named_scope("b3"):
         backward_main(3)
     with jax.named_scope("we"):
         e_cp.wait()
 
+    @pl.when(gx == 1)
+    def _():
+        for k in range(1, HALF):
+            for x in range(2):
+                d_copy(k, x).wait_send()
+
     def shift_of(side):
         return (120 * side - (base + 4 + 4 * side) + 4 * side + 256) % 128
 
@@ -389,15 +466,15 @@
     other_mask = (first & (gx == 1)) | (last & (gx == 0))
 
     def merge(b, _):
-        for i in range(8):
-            j = b * 8 + i
+        for i in range(32):
+            j = b * 32 + i
             z = zof(j)
             v = jnp.where(mine_mask, roll(est[U, j], mine), raw[U, gx, z])
             out_ref[z] = jnp.where(other_mask, roll(erx[j], other), v)
         return 0
 
     with jax.named_scope("merge"):
-        lax.fori_loop(0, NJ // 8, merge, 0)
+        lax.fori_loop(0, NJ // 32, merge, 0)
 
 
 def solution(mesh):
@@ -406,31 +483,34 @@
     vmem = lambda *s: pltpu.VMEM((*s, 8, 128), jnp.float32)
 
     def on_device(u, pc, lc, src, table, rows):
-        hbm = pl.BlockSpec(memory_space=pl.ANY)
-        smem = pl.BlockSpec(memory_space=pltpu.SMEM)
+        hbm = pl.BlockSpec(memory_space=pltpu.HBM)
+        args = [pltpu.with_memory_space_constraint(x, pltpu.HBM) for x in (u, pc, lc, src, table, rows)]
         return pl.pallas_call(
             functools.partial(kernel, ny),
             out_shape=jax.ShapeDtypeStruct(block, jnp.float32),
-            in_specs=[hbm, hbm, hbm, hbm, smem, smem],
+            in_specs=[hbm] * 6,
             out_specs=pl.BlockSpec(memory_space=pltpu.VMEM),
             scratch_shapes=[
                 vmem(4, 2, NJ),
                 vmem(HALF, 2, NJ), vmem(HALF, 2, NJ), vmem(HALF, 2, NJ),
                 vmem(2, NJ), vmem(2, HALF, 2),
-                vmem(HALF, 2), vmem(HALF, 2), vmem(HALF, 2), vmem(HALF, 2),
+                vmem(2, HALF), vmem(2, HALF), vmem(HALF, 2), vmem(HALF, 2),
                 vmem(2, 4, 4), vmem(2, 2, 4, 4), vmem(2, 4, 2), vmem(2, 2, 4, 2),
                 vmem(4, NJ), vmem(HALF, NJ), vmem(HALF, NJ), vmem(HALF, NJ),
                 vmem(NJ), vmem(NJ),
-                pltpu.SemaphoreType.DMA((4,)),
+                pltpu.SMEM((8,), jnp.float32), pltpu.SMEM((HALF,), jnp.int32),
+                pltpu.SemaphoreType.DMA((6,)),
                 pltpu.SemaphoreType.DMA((2, 4)),
                 pltpu.SemaphoreType.DMA((2, 2, 2)),
                 pltpu.SemaphoreType.DMA((2, 2, 2)),
+                pltpu.SemaphoreType.DMA((2, 2)),
+                pltpu.SemaphoreType.DMA((2, 2)),
+                pltpu.SemaphoreType.DMA((3, HALF)),
                 pltpu.SemaphoreType.DMA((2,)),
-                pltpu.SemaphoreType.DMA((2, HALF)),
-                pltpu.SemaphoreType.DMA((2,)),
+                pltpu.SemaphoreType.REGULAR,
             ],
-            compiler_params=pltpu.CompilerParams(collective_id=0, has_side_effects=True),
-        )(u, pc, lc, src, table, rows)
+            compiler_params=pltpu.CompilerParams(collective_id=0, has_side_effects=True, vmem_limit_bytes=24 * 2**20),
+        )(*args)
 
     split = P("gz", "gx", "gy")
     return jax.shard_map(

time: 28.2 us -> 21 us (0.74)
  Pallas kernels: 26.3 us -> 20.2 us
  local copies, waits for them, and re-layouts: 1.67 us -> 0.71 us
    pallas_call x1, Pallas kernels: 26.3 us -> 20.2 us  [on_device(): pl.pallas_call(functools.partial(kernel, ny), out_shape=jax.ShapeDtypeStr...]
    unnamed x1, local copies, waits for them, and re-layouts: 1.67 us -> 0.71 us
where the time goes in v3:
time: 21 us; the launch traced here: 20.9 us
  Pallas kernels  20.2 us (96%)
  local copies, waits for them, and re-layouts  0.71 us (3%)
    pallas_call x1, Pallas kernels, on_device(): pl.pallas_call(functools.partial(kernel, ny), out_shape=jax.ShapeDtypeStr...  20.2 us
    unnamed x1, local copies, waits for them, and re-layouts  0.71 us

profile of v3, /device:TPU:97, one launch (start us, length us, event | category | flops | bytes accessed | tf_op | source)
XLA Modules:
  0.0 20.9 jit_solution(13816435384876987421)
XLA Ops:
  0.0 20.2 %shard_map.64 = f32[64,8,128]{2,1,0:T(8,128)S(1)} custom-call(f32[64,8,128]{2,1,0:T(8,128)} %u_hbm.1, f32[64,8,128]{2,1,0:T(8,128)} %pc_hbm.1, f32[64,8,128]{2,1,0:T(8,128)} %lc_hbm.1, f32[64,8,128]{2,1,0:T(8,128)} %src_hbm.1, f32[8]{0:T(128)} %table_hbm.1, s32[4]{0:T(128)} %rows_hbm.1), custom_call_target="tpu_custom_call" | custom-call | tf_op jit(solution)/shard_map/pallas_call | solution.py:488
  20.2 0.7 %copy.8 = f32[64,8,128]{2,1,0:T(8,128)} copy(f32[64,8,128]{2,1,0:T(8,128)S(1)} %shard_map.64) | data formatting | bytes 524288

commit v4 on v2

v4 whole, which is shorter than its diff:
```python
import functools

import jax
import jax.numpy as jnp
from jax import lax
from jax.experimental import pallas as pl
from jax.experimental.pallas import tpu as pltpu
from jax.sharding import PartitionSpec as P

HALF = 4
NJ = 64
MESH = pl.DeviceIdType.MESH
U, PC, SRC, LC = range(4)
LC_FILL = 4000.0


def kernel(
    ny,
    u_hbm, pc_hbm, lc_hbm, src_hbm, table_hbm, rows_hbm,
    out_ref,
    raw, fac, prv, quo, dsc, mid, gtx, grx, dtx, drx,
    own_pk, own_rx, halo_pk, halo_rx, est, efac, eprv, equo, eds, emid, res_tx, res_rx, pass_rx, fin, fin_rx,
    table, rows, load_sem, raw_sem, own_sem, halo_sem, pass_sem, g_sem, d_sem, last_sem, fin_sem, e_sem, go,
):
    gz, gx, gy = lax.axis_index("gz"), lax.axis_index("gx"), lax.axis_index("gy")
    has_left, has_right = gy > 0, gy < ny - 1
    y_left, y_right = lax.rem(gy + ny - 1, ny), lax.rem(gy + 1, ny)
    lane = lax.broadcasted_iota(jnp.int32, (8, 128), 1)
    row = lax.broadcasted_iota(jnp.int32, (8, 128), 0)
    base = 64 * gx + 32 * gz
    ones = jnp.full((8, 128), 1.0, jnp.float32)
    zero = jnp.zeros((8, 128), jnp.float32)

    def zof(j):
        return jnp.where(gz == 0, j, NJ - 1 - j)

    def remote(src, dst, send, recv, dev):
        return pltpu.make_async_remote_copy(
            src_ref=src, dst_ref=dst, send_sem=send, recv_sem=recv, device_id=dev, device_id_type=MESH
        )

    def roll(v, amount, axis=1):
        return pltpu.roll(v, amount, axis)

    loads = [
        pltpu.make_async_copy(ref, raw.at[a, gx], load_sem.at[a])
        for a, ref in ((LC, lc_hbm), (U, u_hbm), (PC, pc_hbm), (SRC, src_hbm))
    ]
    loads.append(pltpu.make_async_copy(table_hbm, table, load_sem.at[4]))
    loads.append(pltpu.make_async_copy(rows_hbm, rows, load_sem.at[5]))
    for c in loads:
        c.start()
    barrier = pltpu.get_barrier_semaphore()

    def hello(sem, dev):
        pl.semaphore_signal(sem, inc=1, device_id=dev, device_id_type=MESH)

    hello(barrier, (1 - gz, 1, gy))

    @pl.when(gx == 0)
    def _():
        hello(barrier, (gz, 1, gy))

    @pl.when((gx == 0) & (gz == 0) & has_left)
    def _():
        for z in range(2):
            hello(barrier, (z, 0, y_left))

    @pl.when((gx == 0) & (gz == 1) & has_right)
    def _():
        for z in range(2):
            hello(barrier, (z, 0, y_right))

    for c in loads:
        c.wait()

    low_half, even = (lane & 7) < 4, (lane & 8) == 0

    def pack(g, _):
        for a in range(4):
            left, right = [], []
            for h in range(2):
                both = []
                for q in range(2):
                    v = zero
                    for b in range(8):
                        at = 16 * b
                        w = roll(raw[a, gx, zof(g * 32 + h * 16 + q * 8 + b)], (at + 8) % 128)
                        v = w if b == 0 else jnp.where((lane >= at) & (lane < at + 16), w, v)
                    both.append(v)
                left.append(jnp.where(even, roll(both[0], 120), both[1]))
                right.append(jnp.where(even, both[0], roll(both[1], 8)))
            for h in range(2):
                own_pk[0, a, 2 * g + h] = roll(left[h], base + 4)
                own_pk[1, a, 2 * g + h] = roll(right[h], base + 4)
            halo_pk[0, a, g] = roll(jnp.where(low_half, left[0], roll(left[1], 4)), base + 12)
            halo_pk[1, a, g] = roll(jnp.where(low_half, roll(right[0], 124), right[1]), base)
        return 0

    def octet(jj):
        return 8 * (2 * jj if jj < 8 else 2 * (jj - 8) + 1)

    with jax.named_scope("pack"):
        lax.fori_loop(0, 2, pack, 0)

    with jax.named_scope("wait_barrier"):

        @pl.when(gx == 1)
        def _():
            pl.semaphore_wait(barrier, 3)
            hello(go, (gz, 0, gy))

        @pl.when(gx == 0)
        def _():
            pl.semaphore_wait(go, 1)

    raw_cp = {
        a: remote(raw.at[a, 0], raw.at[a, 0], raw_sem.at[0, a], raw_sem.at[1, a], (gz, 1, gy)) for a in (LC, U, PC, SRC)
    }
    pass_cp = remote(halo_pk, pass_rx, pass_sem.at[0], pass_sem.at[1], (gz, 0, gy))

    def halo_copies(side, dev):
        return [
            remote(pk.at[side], halo_rx.at[x, gz], halo_sem.at[0, side, x], halo_sem.at[1, x, gz], dev)
            for x, pk in ((0, halo_pk), (1, pass_rx))
        ]

    def halo_l():
        return halo_copies(0, (1, 0, y_left))

    def halo_r():
        return halo_copies(1, (0, 0, y_right))

    own_far = remote(own_pk.at[1 - gz], own_rx.at[gx, gz], own_sem.at[0, 0, 0], own_sem.at[1, gx, gz], (1 - gz, 0, gy))
    own_near = remote(own_pk.at[gz], own_rx.at[1, gz], own_sem.at[0, 0, 1], own_sem.at[1, 1, gz], (gz, 0, gy))
    g_cp = remote(gtx, grx, g_sem.at[0], g_sem.at[1], (1 - gz, 1, gy))

    def d_copy(k):
        return remote(dtx.at[k], drx.at[k], d_sem.at[0, k], d_sem.at[1, k], (1 - gz, 1, gy))

    def wait_d(k):
        d_copy(k).wait_recv()

    last_copy = remote(dtx.at[HALF - 1, 0], drx.at[HALF - 1, 0], last_sem.at[0], last_sem.at[1], (1 - gz, 0, gy))
    dsc_cp = remote(dsc.at[0], dsc.at[0], fin_sem.at[0, 0], fin_sem.at[1, 0], (gz, 0, gy))
    fin_cp = remote(fin, fin_rx, fin_sem.at[0, 1], fin_sem.at[1, 1], (gz, 0, gy))

    inv = []
    for k in range(HALF):
        shift = jnp.float32(0.0)
        for i in range(table.shape[0]):
            shift = shift + jnp.where(rows[k] == i, table[i], 0.0)
        inv.append(1.0 / jnp.full((8, 128), shift, jnp.float32))

    def factors(load_lc, store):
        def block(b, carry):
            ps, ds, rs = carry
            ps, ds, rs = list(ps), list(ds), list(rs)
            for i in range(16):
                j = b * 16 + i
                t_line = 1.0 / load_lc(j)
                for k in range(HALF):
                    old, r_old = ps[k], rs[k]
                    ds[k] = ds[k] + (t_line * inv[k]) * old
                    ps[k] = old + ds[k]
                    rs[k] = 1.0 / ps[k]
                    store(k, j, t_line * old, old, r_old * rs[k])
            return tuple(ps), tuple(ds), tuple(rs)

        start = (ones,) * HALF
        return lax.fori_loop(0, NJ // 16, block, (start, start, start))

    def main_factors(t):
        def store(k, j, f, p, q):
            z = zof(j)
            fac[k, t, z] = f
            prv[k, t, z] = p
            quo[k, t, z] = q

        ps, ds, rs = factors(lambda j: raw[LC, t, zof(j)], store)
        for k in range(HALF):
            mid[0, k, t] = rs[k]
            gtx[t, k] = ds[k] * rs[k]

    def forward_main(k):
        def block(b, totals):
            totals = list(totals)
            for i in range(32):
                z = zof(b * 32 + i)
                us = [raw[U, 0, z], raw[U, 1, z]]
                down = [roll(u, 1, 0) for u in us]
                up = [roll(u, 7, 0) for u in us]
                low = [jnp.where(row == 0, 0.0, down[0]), jnp.where(row == 0, down[0], down[1])]
                high = [jnp.where(row == 7, up[1], up[0]), jnp.where(row == 7, 0.0, up[1])]
                for t in range(2):
                    beside = (low[t] + high[t]) + (roll(us[t], 1) + roll(us[t], 127))
                    e = inv[k] * us[t] + raw[PC, t, z] * (beside - 4.0 * us[t]) + raw[SRC, t, z]
                    totals[t] = totals[t] + fac[k, t, z] * e
                    dsc[t, z] = totals[t]
            return tuple(totals)

        totals = lax.fori_loop(0, NJ // 32, block, (zero, zero))
        for t in range(2):
            dtx[k, t] = totals[t] * mid[0, k, t]
        d_copy(k).start()
        if k == HALF - 1:
            last_copy.start()

    def backward_main(k):
        last = zof(NJ - 1)
        ys = []
        for t in range(2):
            y = (dtx[k, t] + (1.0 - gtx[t, k]) * drx[k, t]) * mid[1, k, t]
            raw[U, t, last] = prv[k, t, last] * y
            ys.append(y)

        def block(b, ys):
            ys = list(ys)
            for i in range(21):
                z = zof(NJ - 2 - (b * 21 + i))
                for t in range(2):
                    ys[t] = ys[t] + dsc[t, z] * quo[k, t, z]
                    raw[U, t, z] = prv[k, t, z] * ys[t]
            return tuple(ys)

        lax.fori_loop(0, 3, block, tuple(ys))

    quads = [(x, z) for x in range(2) for z in range(2)]
    fills = {U: 0.0, PC: 0.0, SRC: 0.0, LC: LC_FILL}

    def unpack_own():
        def block(g, _):
            for jj in range(16):
                masks = [((lane - (64 * x + 32 * z + 4 + octet(jj))) & 127) < 8 for x, z in quads]
                for a in range(4):
                    v = jnp.full((8, 128), fills[a], jnp.float32)
                    for (x, z), m in zip(quads, masks):
                        v = jnp.where(m, own_rx[x, z, a, g], v)
                    est[a, g * 16 + jj] = roll(v, (-octet(jj)) % 128) if jj else v
            return 0

        lax.fori_loop(0, 4, block, 0)

    def unpack_halo():
        shifted = lane - 12 * gz

        def block(g, _):
            for jj in range(32):
                at = octet(jj) if jj < 16 else octet(jj - 16) + 4
                masks = [((shifted - (64 * x + 32 * z + at)) & 127) < 4 for x, z in quads]
                m_all = (shifted & 31) < 4
                for a in range(4):
                    v = zero
                    for (x, z), m in zip(quads, masks):
                        v = jnp.where(m, halo_rx[x, z, a, g], v)
                    v = roll(v, (-at) % 128) if at else v
                    est[a, g * 32 + jj] = jnp.where(m_all, v, est[a, g * 32 + jj])
            return 0

        lax.fori_loop(0, 2, block, 0)

    def edge_factors():
        def store(k, j, f, p, q):
            efac[k, j] = f
            eprv[k, j] = p
            equo[k, j] = q

        ps, ds, rs = factors(lambda j: est[LC, j], store)
        for k in range(HALF):
            emid[0, k] = ds[k] * rs[k]
            emid[1, k] = rs[k]

    def other_half(v):
        return jnp.where((lane & 32) == 0, roll(v, 96), roll(v, 32))

    def edge_step(k):
        outer_low = (row == 0) & (lane < 64)
        outer_high = (row == 7) & (lane >= 64)

        def fwd(b, total):
            for i in range(32):
                j = b * 32 + i
                u = est[U, j]
                cross = roll(u, 64)
                low = jnp.where(outer_low, 0.0, roll(jnp.where(row == 7, cross, u), 1, 0))
                high = jnp.where(outer_high, 0.0, roll(jnp.where(row == 0, cross, u), 7, 0))
                beside = (low + high) + (roll(u, 1) + roll(u, 127))
                e = inv[k] * u + est[PC, j] * (beside - 4.0 * u) + est[SRC, j]
                total = total + efac[k, j] * e
                eds[j] = total
            return total

        total = lax.fori_loop(0, NJ // 32, fwd, zero)
        d = total * emid[1, k]
        g = emid[0, k]
        last_p = eprv[k, NJ - 1]
        y = (d + (1.0 - g) * other_half(d)) / ((g + other_half(g) * (1.0 - g)) * last_p)
        est[U, NJ - 1] = last_p * y

        def back(b, y):
            for i in range(21):
                j = NJ - 2 - (b * 21 + i)
                y = y + eds[j] * equo[k, j]
                est[U, j] = eprv[k, j] * y
            return y

        lax.fori_loop(0, 3, back, y)

    def pack_result():
        shifted = lane - 4 * gz
        outs = [[zero, zero] for _ in quads]
        for i in range(32):
            us = [est[U, i], est[U, 32 + i]]
            if i:
                us = [roll(u, 4 * i) for u in us]
            for n, (x, z) in enumerate(quads):
                m = ((shifted - (64 * x + 32 * z + 4 + 4 * i)) & 127) < 4
                for h in range(2):
                    outs[n][h] = jnp.where(m, us[h], outs[n][h])
        for n, (x, z) in enumerate(quads):
            for h in range(2):
                res_tx[x, z, h] = roll(outs[n][h], lax.rem(120 * gz + 256 - (64 * x + 32 * z + 4), 128))
        for h in range(2):
            res_rx[gz, h] = res_tx[0, gz, h]

    def res_copy(x, z):
        return remote(res_tx.at[x, z], res_rx.at[gz], e_sem.at[x, z, 0], e_sem.at[2, gz, 0], (z, x, gy))

    def main_problem():
        pass_cp.start()
        own_near.start()
        with jax.named_scope("fac1"):
            main_factors(1)
        with jax.named_scope("wait_lc"):
            raw_cp[LC].wait_recv()
        with jax.named_scope("fac0m"):
            main_factors(0)
        g_cp.start()
        with jax.named_scope("wait_raw"):
            for a in (U, PC, SRC):
                raw_cp[a].wait_recv()
        with jax.named_scope("f0"):
            forward_main(0)
        own_far.start()
        with jax.named_scope("wait_g"):
            g_cp.wait()
        for k in range(HALF):
            for t in range(2):
                g = gtx[t, k]
                mid[1, k, t] = 1.0 / ((g + grx[t, k] * (1.0 - g)) * prv[k, t, zof(NJ - 1)])
        for k in range(1, HALF):
            with jax.named_scope(f"w{k - 1}"):
                wait_d(k - 1)
            with jax.named_scope(f"b{k - 1}"):
                backward_main(k - 1)
            with jax.named_scope(f"f{k}"):
                forward_main(k)
        dsc_cp.start()
        fin[0] = dtx[HALF - 1, 0] * mid[1, HALF - 1, 0]
        fin[1] = (1.0 - gtx[0, HALF - 1]) * mid[1, HALF - 1, 0]
        fin_cp.start()

    def edge_problem():
        for a in range(4):
            for g in range(4):
                own_rx[gx, gz, a, g] = own_pk[gz, a, g]
        with jax.named_scope("fac0"):
            main_factors(0)
        with jax.named_scope("wait_own"):
            for x, z in quads:

                @pl.when((x == 1) | (z != gz))
                def _():
                    remote(own_rx.at[x, z], own_rx.at[x, z], own_sem.at[0, 0, 0], own_sem.at[1, x, z], (gz, 1, gy)).wait_recv()

        with jax.named_scope("unpack_own"):
            unpack_own()

        @pl.when(((gz == 0) & has_left) | ((gz == 1) & has_right))
        def _():
            with jax.named_scope("wait_halo"):
                for x, z in quads:
                    remote(halo_rx.at[x, z], halo_rx.at[x, z], halo_sem.at[0, 0, 0], halo_sem.at[1, x, z], (gz, 1, gy)).wait_recv()
            with jax.named_scope("unpack_halo"):
                unpack_halo()

        with jax.named_scope("edge_fac"):
            edge_factors()
        for k in range(HALF):
            with jax.named_scope(f"e{k}"):
                edge_step(k)
        with jax.named_scope("epack"):
            pack_result()
        for x, z in ((1, 0), (1, 1), (0, 0), (0, 1)):

            @pl.when((x == 1) | (z != gz))
            def _():
                res_copy(x, z).start()

    @pl.when(gx == 1)
    def _():
        main_problem()

    @pl.when(gx == 0)
    def _():
        for c in raw_cp.values():
            c.start()
        with jax.named_scope("wait_pass"):
            pass_cp.wait_recv()
        with jax.named_scope("wait_y"):
            pl.semaphore_wait(barrier, has_left.astype(jnp.int32) + has_right.astype(jnp.int32))

        @pl.when(has_left)
        def _():
            for c in halo_l():
                c.start()

        @pl.when(has_right)
        def _():
            for c in halo_r():
                c.start()

        own_far.start()
        edge_problem()

    with jax.named_scope("we"):
        for side in range(2):

            @pl.when((gx == 1) | (gz != side))
            def _():
                remote(res_rx.at[side], res_rx.at[side], e_sem.at[0, 0, 0], e_sem.at[2, side, 0], (gz, 1 - gx, gy)).wait_recv()

    first, last = lane < 4, lane >= 124

    def finish(t, y):
        k = HALF - 1
        for j in reversed(range(NJ)):
            z, at = zof(j), (-4 * (j % 32)) % 128
            left, right = res_rx[0, j // 32], res_rx[1, j // 32]
            if at:
                left, right = roll(left, at), roll(right, at)
            if j < NJ - 1:
                y = y + dsc[t, z] * quo[k, t, z]
            out_ref[z] = jnp.where(last, right, jnp.where(first, left, prv[k, t, z] * y))

    @pl.when(gx == 1)
    def _():
        k = HALF - 1
        with jax.named_scope("w3"):
            wait_d(k)
        with jax.named_scope("finish"):
            finish(1, (dtx[k, 1] + (1.0 - gtx[1, k]) * drx[k, 1]) * mid[1, k, 1])
        pass_cp.wait_send()
        own_near.wait_send()
        for i in range(HALF):
            d_copy(i).wait_send()
        last_copy.wait_send()
        dsc_cp.wait_send()
        fin_cp.wait_send()

    @pl.when(gx == 0)
    def _():
        with jax.named_scope("w3s"):
            dsc_cp.wait_recv()
            fin_cp.wait_recv()
            last_copy.wait_recv()
        with jax.named_scope("finish_s"):
            finish(0, fin_rx[0] + fin_rx[1] * drx[HALF - 1, 0])
        for c in raw_cp.values():
            c.wait_send()
        for x, z in quads:

            @pl.when((x == 1) | (z != gz))
            def _():
                res_copy(x, z).wait_send()

        @pl.when(has_left)
        def _():
            for c in halo_l():
                c.wait_send()

        @pl.when(has_right)
        def _():
            for c in halo_r():
                c.wait_send()

    own_far.wait_send()


def solution(mesh):
    ny = mesh.shape["gy"]
    block = (NJ, 8, 128)
    vmem = lambda *s: pltpu.VMEM((*s, 8, 128), jnp.float32)

    def on_device(u, pc, lc, src, table, rows):
        hbm = pl.BlockSpec(memory_space=pltpu.HBM)
        args = [pltpu.with_memory_space_constraint(x, pltpu.HBM) for x in (u, pc, lc, src, table, rows)]
        return pl.pallas_call(
            functools.partial(kernel, ny),
            out_shape=jax.ShapeDtypeStruct(block, jnp.float32),
            in_specs=[hbm] * 6,
            out_specs=pl.BlockSpec(memory_space=pltpu.VMEM),
            scratch_shapes=[
                vmem(4, 2, NJ),
                vmem(HALF, 2, NJ), vmem(HALF, 2, NJ), vmem(HALF, 2, NJ),
                vmem(2, NJ), vmem(2, HALF, 2),
                vmem(2, HALF), vmem(2, HALF), vmem(HALF, 2), vmem(HALF, 2),
                vmem(2, 4, 4), vmem(2, 2, 4, 4), vmem(2, 4, 2), vmem(2, 2, 4, 2),
                vmem(4, NJ), vmem(HALF, NJ), vmem(HALF, NJ), vmem(HALF, NJ),
                vmem(NJ), vmem(2, HALF), vmem(2, 2, 2), vmem(2, 2), vmem(2, 4, 2), vmem(2), vmem(2),
                pltpu.SMEM((8,), jnp.float32), pltpu.SMEM((HALF,), jnp.int32),
                pltpu.SemaphoreType.DMA((6,)),
                pltpu.SemaphoreType.DMA((2, 4)),
                pltpu.SemaphoreType.DMA((2, 2, 2)),
                pltpu.SemaphoreType.DMA((2, 2, 2)),
                pltpu.SemaphoreType.DMA((2,)),
                pltpu.SemaphoreType.DMA((2,)),
                pltpu.SemaphoreType.DMA((2, HALF)),
                pltpu.SemaphoreType.DMA((2,)),
                pltpu.SemaphoreType.DMA((2, 2)),
                pltpu.SemaphoreType.DMA((3, 2, 1)),
                pltpu.SemaphoreType.REGULAR,
            ],
            compiler_params=pltpu.CompilerParams(collective_id=0, has_side_effects=True, vmem_limit_bytes=24 * 2**20),
        )(*args)

    split = P("gz", "gx", "gy")
    return jax.shard_map(
        on_device, mesh=mesh, in_specs=(split,) * 4 + (P(), P()), out_specs=split, check_vma=False
    )
```

time: 28.2 us -> 17.6 us (0.62)
  the two profiles are of different devices: /device:TPU:97 before, /device:TPU:98 now
where the time goes in v4:
time: 17.6 us; the launch traced here: 17.4 us
  Pallas kernels  16.7 us (95%)
  local copies, waits for them, and re-layouts  0.71 us (4%)
    pallas_call x1, Pallas kernels, on_device(): pl.pallas_call(functools.partial(kernel, ny), out_shape=jax.ShapeDtypeStr...  16.7 us
    unnamed x1, local copies, waits for them, and re-layouts  0.71 us

profile of v4, /device:TPU:98, one launch (start us, length us, event | category | flops | bytes accessed | tf_op | source)
XLA Modules:
  0.0 17.4 jit_solution(1261132636916830736)
XLA Ops:
  0.0 16.7 %shard_map.64 = f32[64,8,128]{2,1,0:T(8,128)S(1)} custom-call(f32[64,8,128]{2,1,0:T(8,128)} %u_hbm.1, f32[64,8,128]{2,1,0:T(8,128)} %pc_hbm.1, f32[64,8,128]{2,1,0:T(8,128)} %lc_hbm.1, f32[64,8,128]{2,1,0:T(8,128)} %src_hbm.1, f32[8]{0:T(128)} %table_hbm.1, s32[4]{0:T(128)} %rows_hbm.1), custom_call_target="tpu_custom_call" | custom-call | tf_op jit(solution)/shard_map/pallas_call | solution.py:498
  16.7 0.7 %copy.8 = f32[64,8,128]{2,1,0:T(8,128)} copy(f32[64,8,128]{2,1,0:T(8,128)S(1)} %shard_map.64) | data formatting | bytes 524288

commit v5 on v4

--- a/solution.py
+++ b/solution.py
@@ -71,12 +71,41 @@
         for z in range(2):
             hello(barrier, (z, 0, y_right))
 
+    with jax.named_scope("wait_barrier"):
+
+        @pl.when(gx == 1)
+        def _():
+            pl.semaphore_wait(barrier, 3)
+            hello(go, (gz, 0, gy))
+
+        @pl.when(gx == 0)
+        def _():
+            pl.semaphore_wait(go, 1)
+
     for c in loads:
         c.wait()
 
-    low_half, even = (lane & 7) < 4, (lane & 8) == 0
+    raw_cp = {
+        a: remote(raw.at[a, 0], raw.at[a, 0], raw_sem.at[0, a], raw_sem.at[1, a], (gz, 1, gy)) for a in (LC, U, PC, SRC)
+    }
+
+    @pl.when(gx == 0)
+    def _():
+        for c in raw_cp.values():
+            c.start()
+
+
+    spot = (lane - base - 4) & 127
+    low_half, even = (spot & 7) < 4, (spot & 8) == 0
+    group = jnp.where(gz == 0, spot >> 4, 7 - (spot >> 4))
+    places = [(base + 12 + jnp.where(gz == 0, 16 * b, 112 - 16 * b)) & 127 for b in range(8)]
+    forwards = jnp.full((8, 128), gz, jnp.int32) == 0
+
+    def in_order(pair):
+        return jnp.where(forwards, pair[0], pair[1]), jnp.where(forwards, pair[1], pair[0])
 
     def pack(g, _):
+        at = jnp.where(gz == 0, g, 1 - g)
         for a in range(4):
             left, right = [], []
             for h in range(2):
@@ -84,17 +113,18 @@
                 for q in range(2):
                     v = zero
                     for b in range(8):
-                        at = 16 * b
-                        w = roll(raw[a, gx, zof(g * 32 + h * 16 + q * 8 + b)], (at + 8) % 128)
-                        v = w if b == 0 else jnp.where((lane >= at) & (lane < at + 16), w, v)
+                        w = roll(raw[a, gx, g * 32 + (h * 16 + q * 8 + b)], places[b])
+                        v = w if b == 0 else jnp.where(group == b, w, v)
                     both.append(v)
+                both = in_order(both)
                 left.append(jnp.where(even, roll(both[0], 120), both[1]))
                 right.append(jnp.where(even, both[0], roll(both[1], 8)))
+            left, right = in_order(left), in_order(right)
             for h in range(2):
-                own_pk[0, a, 2 * g + h] = roll(left[h], base + 4)
-                own_pk[1, a, 2 * g + h] = roll(right[h], base + 4)
-            halo_pk[0, a, g] = roll(jnp.where(low_half, left[0], roll(left[1], 4)), base + 12)
-            halo_pk[1, a, g] = roll(jnp.where(low_half, roll(right[0], 124), right[1]), base)
+                own_pk[0, a, 2 * at + h] = left[h]
+                own_pk[1, a, 2 * at + h] = right[h]
+            halo_pk[0, a, at] = jnp.where(low_half, roll(left[0], 8), roll(left[1], 12))
+            halo_pk[1, a, at] = jnp.where(low_half, roll(right[1], 124), roll(right[0], 120))
         return 0
 
     def octet(jj):
@@ -103,33 +133,11 @@
     with jax.named_scope("pack"):
         lax.fori_loop(0, 2, pack, 0)
 
-    with jax.named_scope("wait_barrier"):
-
-        @pl.when(gx == 1)
-        def _():
-            pl.semaphore_wait(barrier, 3)
-            hello(go, (gz, 0, gy))
-
-        @pl.when(gx == 0)
-        def _():
-            pl.semaphore_wait(go, 1)
-
-    raw_cp = {
-        a: remote(raw.at[a, 0], raw.at[a, 0], raw_sem.at[0, a], raw_sem.at[1, a], (gz, 1, gy)) for a in (LC, U, PC, SRC)
-    }
     pass_cp = remote(halo_pk, pass_rx, pass_sem.at[0], pass_sem.at[1], (gz, 0, gy))
 
-    def halo_copies(side, dev):
-        return [
-            remote(pk.at[side], halo_rx.at[x, gz], halo_sem.at[0, side, x], halo_sem.at[1, x, gz], dev)
-            for x, pk in ((0, halo_pk), (1, pass_rx))
-        ]
-
-    def halo_l():
-        return halo_copies(0, (1, 0, y_left))
-
-    def halo_r():
-        return halo_copies(1, (0, 0, y_right))
+    def halo_copy(x, side):
+        pk, dev = (halo_pk, pass_rx)[x], ((1, 0, y_left), (0, 0, y_right))[side]
+        return remote(pk.at[side], halo_rx.at[x, gz], halo_sem.at[0, side, x], halo_sem.at[1, x, gz], dev)
 
     own_far = remote(own_pk.at[1 - gz], own_rx.at[gx, gz], own_sem.at[0, 0, 0], own_sem.at[1, gx, gz], (1 - gz, 0, gy))
     own_near = remote(own_pk.at[gz], own_rx.at[1, gz], own_sem.at[0, 0, 1], own_sem.at[1, 1, gz], (gz, 0, gy))
@@ -185,8 +193,8 @@
     def forward_main(k):
         def block(b, totals):
             totals = list(totals)
-            for i in range(32):
-                z = zof(b * 32 + i)
+            for i in range(64):
+                z = zof(i)
                 us = [raw[U, 0, z], raw[U, 1, z]]
                 down = [roll(u, 1, 0) for u in us]
                 up = [roll(u, 7, 0) for u in us]
@@ -199,7 +207,7 @@
                     dsc[t, z] = totals[t]
             return tuple(totals)
 
-        totals = lax.fori_loop(0, NJ // 32, block, (zero, zero))
+        totals = block(0, (zero, zero))
         for t in range(2):
             dtx[k, t] = totals[t] * mid[0, k, t]
         d_copy(k).start()
@@ -278,8 +286,8 @@
         outer_high = (row == 7) & (lane >= 64)
 
         def fwd(b, total):
-            for i in range(32):
-                j = b * 32 + i
+            for i in range(64):
+                j = i
                 u = est[U, j]
                 cross = roll(u, 64)
                 low = jnp.where(outer_low, 0.0, roll(jnp.where(row == 7, cross, u), 1, 0))
@@ -290,21 +298,16 @@
                 eds[j] = total
             return total
 
-        total = lax.fori_loop(0, NJ // 32, fwd, zero)
+        total = fwd(0, zero)
         d = total * emid[1, k]
         g = emid[0, k]
         last_p = eprv[k, NJ - 1]
         y = (d + (1.0 - g) * other_half(d)) / ((g + other_half(g) * (1.0 - g)) * last_p)
         est[U, NJ - 1] = last_p * y
 
-        def back(b, y):
-            for i in range(21):
-                j = NJ - 2 - (b * 21 + i)
-                y = y + eds[j] * equo[k, j]
-                est[U, j] = eprv[k, j] * y
-            return y
-
-        lax.fori_loop(0, 3, back, y)
+        for j in reversed(range(NJ - 1)):
+            y = y + eds[j] * equo[k, j]
+            est[U, j] = eprv[k, j] * y
 
     def pack_result():
         shifted = lane - 4 * gz
@@ -403,23 +406,14 @@
 
     @pl.when(gx == 0)
     def _():
-        for c in raw_cp.values():
-            c.start()
-        with jax.named_scope("wait_pass"):
-            pass_cp.wait_recv()
         with jax.named_scope("wait_y"):
             pl.semaphore_wait(barrier, has_left.astype(jnp.int32) + has_right.astype(jnp.int32))
-
-        @pl.when(has_left)
-        def _():
-            for c in halo_l():
-                c.start()
-
-        @pl.when(has_right)
-        def _():
-            for c in halo_r():
-                c.start()
-
+        for x in range(2):
+            if x:
+                with jax.named_scope("wait_pass"):
+                    pass_cp.wait_recv()
+            for side, there in enumerate((has_left, has_right)):
+                pl.when(there)(halo_copy(x, side).start)
         own_far.start()
         edge_problem()
 
@@ -474,15 +468,9 @@
             def _():
                 res_copy(x, z).wait_send()
 
-        @pl.when(has_left)
-        def _():
-            for c in halo_l():
-                c.wait_send()
-
-        @pl.when(has_right)
-        def _():
-            for c in halo_r():
-                c.wait_send()
+        for x in range(2):
+            for side, there in enumerate((has_left, has_right)):
+                pl.when(there)(halo_copy(x, side).wait_send)
 
     own_far.wait_send()
 

time: 17.6 us -> 16.5 us (0.937)
  the two profiles are of different devices: /device:TPU:98 before, /device:TPU:97 now
where the time goes in v5:
time: 16.5 us; the launch traced here: 16.2 us
  Pallas kernels  15.5 us (94%)
  local copies, waits for them, and re-layouts  0.71 us (4%)
    pallas_call x1, Pallas kernels, on_device(): pl.pallas_call(functools.partial(kernel, ny), out_shape=jax.ShapeDtypeStr...  15.5 us
    unnamed x1, local copies, waits for them, and re-layouts  0.71 us

profile of v5, /device:TPU:97, one launch (start us, length us, event | category | flops | bytes accessed | tf_op | source)
XLA Modules:
  0.0 16.2 jit_solution(9162496117231542653)
XLA Ops:
  0.0 15.5 %shard_map.64 = f32[64,8,128]{2,1,0:T(8,128)S(1)} custom-call(f32[64,8,128]{2,1,0:T(8,128)} %u_hbm.1, f32[64,8,128]{2,1,0:T(8,128)} %pc_hbm.1, f32[64,8,128]{2,1,0:T(8,128)} %lc_hbm.1, f32[64,8,128]{2,1,0:T(8,128)} %src_hbm.1, f32[8]{0:T(128)} %table_hbm.1, s32[4]{0:T(128)} %rows_hbm.1), custom_call_target="tpu_custom_call" | custom-call | tf_op jit(solution)/shard_map/pallas_call | solution.py:486
  15.5 0.7 %copy.8 = f32[64,8,128]{2,1,0:T(8,128)} copy(f32[64,8,128]{2,1,0:T(8,128)S(1)} %shard_map.64) | data formatting | bytes 524288
